TPU v7x, 32 devices: a 4x4x1 block of a 4x4x8 slice. The times are simulated.
32 devices in a mesh: dp: 1 (over z), cx: 4 (over y), cy: 4 (over x), cz: 2 (over core).
Axes of the slice: x: 4, y: 4, z: 1, core: 2. Of those that a mesh axis runs over, the one named last changes fastest.
The devices are a block of a 4x4x8 slice.
Arguments:
- q: bfloat16 [2048, 64, 128], P(('dp', 'cx', 'cy', 'cz'))
- k: bfloat16 [2048, 8, 128], P(('dp', 'cx', 'cy', 'cz'))
- v: bfloat16 [2048, 8, 128], P(('dp', 'cx', 'cy', 'cz'))
Outputs:
- output: bfloat16 [2048, 64, 128], P(('dp', 'cx', 'cy', 'cz'))
All inputs are finite; a program needn't handle non-finite values.
Results may differ from a plain program's by a relative error of at most 0.00642288.
Values are sent between devices in bfloat16 or wider.
A program may use at most 768 MiB of HBM per device.

v0:
```python
import jax
import jax.numpy as jnp
from jax import lax
from jax.sharding import PartitionSpec as P

NEG = -1e30


def _blocks(t, work):
    c = 1
    while t % (2 * c) == 0 and (work > c << 25 or (c < 8 and work >= c << 22)):
        c *= 2
    return c


def _lead(x, n):
    return jnp.swapaxes(x.reshape((n, -1) + x.shape[1:]), 0, 1).reshape(x.shape)


def _partial(q, k, v, qpos, kpos, lo=0):
    na, t, hq, d = q.shape
    nk, hkvv, _ = k.shape
    g = hq // hkvv
    w = nk // (lo + t)
    n = _blocks(t, hq * na * t * nk)
    c = t // n
    scale = d ** -0.5
    q = q.reshape(na, t, hkvv, g, d)
    outs, lses = [], []
    for j in range(n):
        r0, r1 = j * c, (j + 1) * c
        e = (lo + r1) * w
        s = jnp.einsum('aqhgd,khd->haqgk', q[:, r0:r1], k[:e], preferred_element_type=jnp.float32)
        mask = kpos[:e] <= qpos[:, r0:r1, None]
        s = jnp.where(mask[None, :, :, None, :], s * scale, NEG)
        m = jnp.max(s, axis=-1)
        p = jnp.exp(s - m[..., None])
        l = jnp.transpose(jnp.sum(p, axis=-1), (1, 2, 0, 3))
        m = jnp.transpose(m, (1, 2, 0, 3))
        o = jnp.einsum('haqgk,khd->aqhgd', p.astype(jnp.bfloat16), v[:e], preferred_element_type=jnp.float32)
        ok = m > NEG
        outs.append(o / jnp.where(ok, l, jnp.inf)[..., None])
        lses.append(jnp.where(ok, m + jnp.log(l), NEG))
    o = jnp.concatenate(outs, axis=1) if n > 1 else outs[0]
    lse = jnp.concatenate(lses, axis=1) if n > 1 else lses[0]
    return o.reshape(na, t, hq, d), lse.reshape(na, t, hq)


def solution(mesh):
    a = mesh.shape['cx']
    nz = mesh.shape['cz']
    b = mesh.shape['cy'] * nz
    dev = a * b
    spec = P(('dp', 'cx', 'cy', 'cz'))

    def local(q, k, v):
        t, hq, d = q.shape
        ix = lax.axis_index('cx')
        own = lax.axis_index('cy') * nz + lax.axis_index('cz')
        i = jnp.arange(t, dtype=jnp.int32)
        qpos = i[None, :] * dev + jnp.arange(a, dtype=jnp.int32)[:, None] * b + own
        kpos = (i[:, None] * dev + ix * b + jnp.arange(b, dtype=jnp.int32)[None, :]).reshape(-1)
        qg = lax.all_gather(q, 'cx', axis=0, tiled=True)
        kg = lax.all_gather(k, ('cy', 'cz'), axis=0, tiled=True)
        vg = lax.all_gather(v, ('cy', 'cz'), axis=0, tiled=True)
        o, lse = _partial(qg.reshape(a, t, hq, d), _lead(kg, b), _lead(vg, b), qpos, kpos)
        o = o.reshape(a * t, hq, d)
        lse = lse.reshape(a * t, hq)
        top = lax.pmax(lse, 'cx')
        tot = top + jnp.log(lax.psum(jnp.exp(lse - top), 'cx'))
        o = o * jnp.exp(lse - tot)[..., None]
        return lax.psum_scatter(o, 'cx', scatter_dimension=0, tiled=True).astype(jnp.bfloat16)

    return jax.shard_map(local, mesh=mesh, in_specs=(spec, spec, spec), out_specs=spec, check_vma=False)
```

profile of v0, /device:TPU:97, one launch (start us, length us, event | category | flops | bytes accessed | tf_op | source)
XLA Modules:
  0.0 305.8 jit_solution(3113071423197461762)
XLA Ops:
  6.6 0.7 all-gather.6.cloned.1.call-update
  7.4 0.7 all-gather.8.cloned.1.call-update
  8.2 0.7 all-gather.4.cloned.1.call-update
  10.0 23.9 %all-gather.6.cloned.1.call-done = bf16[512,8,128]{2,1,0:T(8,128)(2,1)} async-done(((bf16[64,8,128]{2,1,0:T(8,128)(2,1)}), bf16[512,8,128]{2,1,0:T(8,128)(2,1)}) %all-gather.6.cloned.1.call-update) | async-done | bytes 1048592 | tf_op jit(solution)/shard_map/all_gather | solution.py:64
  33.9 1.9 copy.94
  35.8 20.1 %all-gather.8.cloned.1.call-done = bf16[512,8,128]{2,1,0:T(8,128)(2,1)} async-done(((bf16[64,8,128]{2,1,0:T(8,128)(2,1)}), bf16[512,8,128]{2,1,0:T(8,128)(2,1)}) %all-gather.8.cloned.1.call-update) | async-done | bytes 1048592 | tf_op jit(solution)/shard_map/all_gather | solution.py:65
  55.9 1.9 copy.93
  57.8 44.5 %all-gather.4.cloned.1.call-done = bf16[256,64,128]{2,1,0:T(8,128)(2,1)} async-done(((bf16[64,64,128]{2,1,0:T(8,128)(2,1)}), bf16[256,64,128]{2,1,0:T(8,128)(2,1)}) %all-gather.4.cloned.1.call-update) | async-done | bytes 4194320 | tf_op jit(solution)/shard_map/all_gather | solution.py:63
  102.3 3.2 %fusion.69 = (bf16[4,16,8,8,128]{4,3,2,1,0:T(8,128)(2,1)S(1)}, bf16[4,16,8,8,128]{4,3,2,1,0:T(8,128)(2,1)S(1)}, bf16[4,16,8,8,128]{4,3,2,1,0:T(8,128)(2,1)S(1)}, bf16[4,16,8,8,128]{4,3,2,1,0:T(8,128)(2,1)S(1)}) fusion(bf16[4,64,8,8,128]{4,3,2,1,0:T(8,128)(2,1)} %bitcast.146), kind=kLoop, calls=%fused_computation.105 | loop fusion | bytes 8388608 | tf_op jit(solution)/shard_map/slice | solution.py:33
  105.5 3.1 %fusion = (f32[8,4,16,8]{3,2,1,0:T(8,128)S(1)}, f32[8,4,16,8,512]{4,3,2,1,0:T(8,128)S(1)}) fusion(pred[4,16,512]{2,1,0:T(8,128)(4,1)S(1)} %broadcast_compare_fusion, bf16[8,64,8,128]{3,2,1,0:T(8,128)(2,1)S(1)} %bitcast.148, bf16[4,16,8,8,128]{4,3,2,1,0:T(8,128)(2,1)S(1)} %get-tuple-element.8), kind=kOutput, calls=%fused_computation.3 | convolution fusion | flops 543158272 | bytes 10534912 | tf_op jit(solution)/shard_map/aqhgd,khd->haqgk/dot_general | solution.py:33
  108.7 2.7 fusion.1
  111.3 1.6 fusion.3
  112.9 2.0 fusion.4
  115.1 4.9 %bitcast_divide_fusion = f32[4,16,8,8,128]{4,3,1,0,2:T(8,128)} fusion(f32[8,4,16,8,512]{4,3,2,1,0:T(8,128)S(1)} %get-tuple-element.22, f32[8,4,16,8]{3,2,1,0:T(8,128)S(1)} %get-tuple-element.21, pred[4,16,512]{2,1,0:T(8,128)(4,1)S(1)} %broadcast_compare_fusion, f32[4,16,8,8]{3,1,0,2:T(8,128)S(1)} %get-tuple-element.16, bf16[8,64,8,128]{3,2,1,0:T(8,128)(2,1)S(1)} %bitcast.150), kind=kOutput, calls=%fused_computation.28 | convolution fusion | flops 545783808 | bytes 11599872 | tf_op jit(solution)/shard_map/haqgk,khd->aqhgd/dot_general | solution.py:40
  120.1 3.5 %bitcast_divide_fusion.1 = f32[4,16,8,8,128]{4,3,1,0,2:T(8,128)} fusion(f32[8,4,16,8,384]{4,3,2,1,0:T(8,128)S(1)} %get-tuple-element.24, f32[8,4,16,8]{3,2,1,0:T(8,128)S(1)} %get-tuple-element.23, pred[4,16,384]{2,1,0:T(8,128)(4,1)S(1)} %broadcast_compare_fusion.1, f32[4,16,8,8]{3,1,0,2:T(8,128)S(1)} %get-tuple-element.29, ...), kind=kOutput, calls=%fused_computation.29 | convolution fusion | flops 409468928 | bytes 9723904 | tf_op jit(solution)/shard_map/haqgk,khd->aqhgd/dot_general | solution.py:40
  123.5 1.0 fusion.12
  124.5 1.6 fusion.13
  126.2 0.8 fusion.27
  127.0 1.4 fusion.32
  128.4 0.8 fusion.58
  129.2 3.0 bitcast_divide_fusion.2
  132.7 0.8 reshape_reshape.11
  133.6 3.3 %bitcast_divide_fusion.3 = f32[4,16,8,8,128]{4,3,1,0,2:T(8,128)} fusion(f32[8,4,16,8,128]{4,3,2,1,0:T(8,128)S(1)} %get-tuple-element.28, f32[4,16,8,8]{3,1,0,2:T(8,128)} %get-tuple-element.31, f32[8,4,16,8]{3,2,1,0:T(8,128)S(1)} %get-tuple-element.27, pred[4,16,128]{2,1,0:T(8,128)(4,1)S(1)} %broadcast_compare_fusion.3, bf16[64,8,8,128]{3,1,0,2:T(8,128)(2,1)} %bitcast.152), kind=kOutput, calls=%fused_computation.31 | convolution fusion | flops 136839168 | bytes 4743168 | tf_op jit(solution)/shard_map/haqgk,khd->aqhgd/dot_general | solution.py:40
  136.9 31.5 %all-reduce.3.cloned.1.call-done = f32[256,64]{0,1:T(8,128)} async-done(((f32[256,64]{0,1:T(8,128)}), f32[256,64]{0,1:T(8,128)}) %all-reduce.3.cloned.1.call-update) | async-done | bytes 65552 | tf_op jit(solution)/shard_map/pmax | solution.py:69
  168.4 1.5 subtract_exponential_fusion.5
  170.0 3.9 %pad_maximum_fusion = f32[4,64,8,8,128]{4,3,1,0,2:T(8,128)S(1)} fusion(f32[4,16,8,8,128]{4,3,1,0,2:T(8,128)} %bitcast_divide_fusion, f32[4,16,8,8,128]{4,3,1,0,2:T(8,128)} %bitcast_divide_fusion.1, f32[4,16,8,8,128]{4,3,1,0,2:T(8,128)} %bitcast_divide_fusion.2, f32[4,16,8,8,128]{4,3,1,0,2:T(8,128)} %bitcast_divide_fusion.3), kind=kLoop, calls=%fused_computation | loop fusion | flops 6291456 | bytes 16777216 | tf_op jit(solution)/shard_map/concatenate | solution.py:44
  173.9 4.4 %copy.50 = f32[4,64,8,8,128]{4,3,2,1,0:T(8,128)} copy(f32[4,64,8,8,128]{4,3,1,0,2:T(8,128)S(1)} %pad_maximum_fusion) | data formatting | bytes 16777216 | tf_op jit(solution)/shard_map/concatenate | solution.py:44
  178.3 28.7 %all-reduce.5.cloned.1.call-done = f32[256,64]{0,1:T(8,128)} async-done(((f32[256,64]{0,1:T(8,128)}), f32[256,64]{0,1:T(8,128)}) %all-reduce.5.cloned.1.call-update) | async-done | bytes 65552 | tf_op jit(solution)/shard_map/psum | solution.py:70
  207.0 0.9 subtract_exponential_fusion.4
  208.0 7.9 %broadcast_multiply_fusion = f32[256,64,128]{2,1,0:T(8,128)} fusion(f32[256,64,128]{2,1,0:T(8,128)} %bitcast.142, f32[256,64]{1,0:T(8,128)S(1)} %copy.52), kind=kLoop, calls=%fused_computation.12 | loop fusion | flops 2097152 | bytes 16842752 | tf_op jit(solution)/shard_map/mul | solution.py:71
  215.9 80.3 %reduce-scatter.2.cloned.1.call-done = f32[64,64,128]{2,1,0:T(8,128)} async-done(((f32[256,64,128]{2,1,0:T(8,128)}), f32[64,64,128]{2,1,0:T(8,128)}) %reduce-scatter.2.cloned.1.call-update) | async-done | bytes 2097168 | tf_op jit(solution)/shard_map/reduce_scatter | solution.py:72
  296.2 2.8 convert_element_type.19
  (42 shorter events, 2.1 us)
Async XLA Ops:
  6.5 27.3 %all-gather.6.cloned.1.call-start = ((), (), s32[]{:S(2)}) async-start(), calls=%async_computation.2 | async-start | bytes 1179648 | tf_op jit(solution)/shard_map/all_gather | solution.py:64
  7.3 48.6 %all-gather.8.cloned.1.call-start = ((), (), s32[]{:S(2)}) async-start(), calls=%async_computation.3 | async-start | bytes 1179648 | tf_op jit(solution)/shard_map/all_gather | solution.py:65
  8.1 94.2 %all-gather.4.cloned.1.call-start = ((), (), s32[]{:S(2)}) async-start(), calls=%async_computation.1 | async-start | bytes 5242880 | tf_op jit(solution)/shard_map/all_gather | solution.py:63
  8.9 159.5 %all-reduce.3.cloned.1.call-start = ((), (), s32[]{:S(2)}) async-start(), calls=%async_computation.4 | async-start | bytes 131072 | tf_op jit(solution)/shard_map/pmax | solution.py:69
  57.8 62.3 %copy-start.3 = (bf16[8,64,8,128]{3,0,1,2:T(8,128)(2,1)}, bf16[8,64,8,128]{3,0,1,2:T(8,128)(2,1)S(1)}, u32[]{:S(2)}) copy-start(bf16[8,64,8,128]{3,0,1,2:T(8,128)(2,1)S(1)} %copy.93) | copy-start | bytes 3145732
  102.3 3.2 %copy-start = (bf16[512,8,128]{2,1,0:T(8,128)(2,1)S(1)}, bf16[512,8,128]{2,1,0:T(8,128)(2,1)}, u32[]{:S(2)}) copy-start(bf16[512,8,128]{2,1,0:T(8,128)(2,1)} %all-gather.6.cloned.1.call-done) | copy-start | bytes 3145732
  112.9 2.2 copy-start.2
  126.2 3.0 copy-start.4
  133.5 73.5 %all-reduce.5.cloned.1.call-start = ((), (), s32[]{:S(2)}) async-start(), calls=%async_computation.5 | async-start | bytes 131072 | tf_op jit(solution)/shard_map/psum | solution.py:70
  133.6 34.8 %copy-start.1 = (f32[256,64]{0,1:T(8,128)S(1)}, f32[256,64]{0,1:T(8,128)}, u32[]{:S(2)}) copy-start(f32[256,64]{0,1:T(8,128)} %reshape_reshape.11) | copy-start | bytes 196612
  169.9 126.3 %reduce-scatter.2.cloned.1.call-start = ((), (), s32[]{:S(2)}) async-start(), calls=%async_computation.6 | async-start | bytes 10485760 | tf_op jit(solution)/shard_map/reduce_scatter | solution.py:72
  173.9 33.1 %copy-start.5 = (f32[256,64]{0,1:T(8,128)S(1)}, f32[256,64]{0,1:T(8,128)}, u32[]{:S(2)}) copy-start(f32[256,64]{0,1:T(8,128)} %all-reduce.3.cloned.1.call-done) | copy-start | bytes 196612
Sparse Core Ops, SparseCore 0:
  9.0 24.8 all-gather.5
  35.5 20.3 all-gather.7
  57.5 44.7 all-gather.3
  133.6 34.7 all-reduce.2
  170.5 36.4 all-reduce.4
  216.0 80.1 reduce-scatter.1
where the time goes:
time: 306 us
  waiting for transfers between devices  231 us (75%)
  other arithmetic  26.2 us (9%)
  matrix products  21.2 us (7%)
  between operations  13.7 us (4%)
  local copies, waits for them, and re-layouts  13.1 us (4%)
    reduce_scatter x1, waiting for transfers between devices, local(): lax.psum_scatter(o, 'cx', scatter_dimension=0, tiled=True)  80.3 us
    all_gather x1, waiting for transfers between devices, local(): qg = lax.all_gather(q, 'cx', axis=0, tiled=True)  44.5 us
    pmax x1, waiting for transfers between devices, local(): top = lax.pmax(lse, 'cx')  31.5 us
    psum x1, waiting for transfers between devices, local(): tot = top + jnp.log(lax.psum(jnp.exp(lse - top), 'cx'))  28.7 us
    all_gather x1, waiting for transfers between devices, local(): kg = lax.all_gather(k, ('cy', 'cz'), axis=0, tiled=True)  23.9 us
    all_gather x1, waiting for transfers between devices, local(): vg = lax.all_gather(v, ('cy', 'cz'), axis=0, tiled=True)  20.1 us
    dot_general x4, matrix products, _partial(): jnp.einsum('haqgk,khd->aqhgd', p.astype(jnp.bfloat16), v[:e], preferred_e...  14.7 us
    mul x1, other arithmetic, local(): o = o * jnp.exp(lse - tot)[..., None]  7.89 us
  transfers between devices with their start and end apart: 6, of which 6 were waited for; matrix products, arithmetic and copies ran while one was open for 5% of the time, Pallas kernels for 0%

commit v1 on v0

v1 whole, which is shorter than its diff:
```python
import functools
import math

import jax
import jax.numpy as jnp
from jax import lax
from jax.experimental import pallas as pl
from jax.experimental.pallas import tpu as pltpu
from jax.sharding import PartitionSpec as P

NEG = -1e30
RING = 4
LINKS = (("x", 1), ("x", -1), ("y", 1), ("y", -1))
HEAD_OF = {("x", 1): 0, ("x", -1): 1, ("y", 1): 2, ("y", -1): 3}
PLAN = (
    ("a", -1), ("b", -1), ("c", -1), ("d", -1), ("a", 0), ("c", 0), ("c", 1), ("d", 1),
    ("c", 4), ("c", 2), ("c", 5), ("c", 6), ("d", 0), ("c", 8), ("d", 4),
)
SLOTS = len(PLAN)
AHEAD = 4


def _head(link, letter):
    axis, sign = link
    other = "y" if axis == "x" else "x"
    return HEAD_OF[{"a": (axis, sign), "b": (axis, -sign), "c": (other, sign), "d": (other, -sign)}[letter]]


def _offsets():
    off = [dict() for _ in range(SLOTS)]
    for slot, (letter, src) in enumerate(PLAN):
        for link in LINKS:
            head = _head(link, letter)
            x, y = (0, 0) if src < 0 else off[src][head]
            axis, sign = link
            x, y = (x + sign, y) if axis == "x" else (x, y + sign)
            assert head not in off[slot]
            off[slot][head] = (x % RING, y % RING)
    for head in range(len(LINKS)):
        assert len({off[s][head] for s in range(SLOTS)} | {(0, 0)}) == RING * RING
    return off


OFF = _offsets()


def _kernel(k_hbm, v_hbm, q_hbm, o_hbm, kin, vin, st, kv, qs, qt, acc, m_ref, l_ref, ost, src,
            in_sem, x_sem, send_sem, recv_sem, out_sem):
    t, hkv, d = k_hbm.shape
    g = q_hbm.shape[2]
    hh = hkv // 2
    nb = t // 16
    w = 2 * 16 * g
    iy, ix, iz = lax.axis_index("cx"), lax.axis_index("cy"), lax.axis_index("cz")
    oz = 1 - iz
    chip = iy * RING + ix
    c = d ** -0.5 * math.log2(math.e)

    def peer(link):
        axis, sign = link
        if axis == "x":
            return {"cy": lax.rem(ix + sign + RING, RING)}
        return {"cx": lax.rem(iy + sign + RING, RING)}

    half = lambda z: pl.ds(pl.multiple_of(z * t, t), t)

    barrier = pltpu.get_barrier_semaphore()
    for link in LINKS:
        pl.semaphore_signal(barrier, inc=1, device_id=peer(link), device_id_type=pl.DeviceIdType.MESH)
    pl.semaphore_signal(barrier, inc=1, device_id={"cz": oz}, device_id_type=pl.DeviceIdType.MESH)
    k_in = pltpu.make_async_copy(k_hbm, kin, in_sem.at[0])
    v_in = pltpu.make_async_copy(v_hbm, vin, in_sem.at[1])
    q_in = pltpu.make_async_copy(q_hbm.at[:, pl.ds(hh * iz, hh)], qs.at[iz], in_sem.at[2])
    k_in.start()
    v_in.start()
    q_in.start()

    for n, (ref, copy) in enumerate(((kin, k_in), (vin, v_in))):
        copy.wait()
        x = jnp.swapaxes(ref[...].astype(jnp.float32), 0, 1)
        st[:, n] = x.astype(jnp.bfloat16)
    for h in range(hh):
        kv[0, h, :, half(iz), :] = st[hh * iz + h]

    def remote(a, b, s, r, to):
        return pltpu.make_async_remote_copy(
            src_ref=a, dst_ref=b, send_sem=s, recv_sem=r, device_id=to, device_id_type=pl.DeviceIdType.MESH)

    def unit(n, slot):
        link = LINKS[n]
        letter, arrival = PLAN[slot]
        h = _head(link, letter)
        sems = send_sem.at[n, slot], recv_sem.at[n, slot], peer(link)
        if slot < 2:
            return remote(st.at[hh * iz + h], kv.at[1 + slot, h, :, half(iz), :], *sems)
        return remote(kv.at[1 + arrival, h], kv.at[1 + slot, h], *sems)

    def rest(n, slot):
        link = LINKS[n]
        h = _head(link, PLAN[slot][0])
        return remote(kv.at[0, h, :, half(oz), :], kv.at[1 + slot, h, :, half(oz), :],
                      send_sem.at[n, SLOTS + slot], recv_sem.at[n, SLOTS + slot], peer(link))

    swap = remote(st.at[pl.ds(hh * oz, hh)], kv.at[0, :, :, half(iz), :], x_sem.at[0], x_sem.at[1], {"cz": oz})
    q_swap = remote(q_hbm.at[:, pl.ds(hh * oz, hh)], qs.at[iz], x_sem.at[2], x_sem.at[3], {"cz": oz})

    pl.semaphore_wait(barrier, len(LINKS) + 1)
    swap.start()
    for slot in range(2):
        for n in range(4):
            unit(n, slot).start()
    q_swap.start()
    swap.wait_recv()
    for slot in range(2):
        for n in range(4):
            rest(n, slot).start()
    for slot in range(2, AHEAD):
        for n in range(4):
            unit(n, slot).start()

    m_ref[...] = jnp.full_like(m_ref, NEG)
    l_ref[...] = jnp.zeros_like(l_ref)
    acc[...] = jnp.zeros_like(acc)

    def turn(p):
        @pl.loop(0, hh)
        def _(h):
            for a in range(nb):
                x = qs[p, 16 * a:16 * (a + 1), h].astype(jnp.float32).reshape(16 * g, d)
                qt[h, a, p] = x.T.astype(jnp.bfloat16)

    q_in.wait()
    q_swap.wait_recv()
    for p in range(2):
        turn(p)

    def step(k, carry):
        @pl.when(k == 0)
        def _():
            for h in range(hh):
                src[h] = chip

        for j in range(1, SLOTS + 1):
            @pl.when(k == j)
            def _():
                for n in range(4):
                    unit(n, j - 1).wait_recv()
                    if j - 1 < 2:
                        rest(n, j - 1).wait_recv()
                if j - 1 + AHEAD < SLOTS:
                    for n in range(4):
                        unit(n, j - 1 + AHEAD).start()
                for h in range(hh):
                    ox, oy = OFF[j - 1][h]
                    src[h] = lax.rem(iy - oy + RING, RING) * RING + lax.rem(ix - ox + RING, RING)

        lane = lax.broadcasted_iota(jnp.int32, (16, w), 1)
        row = lax.broadcasted_iota(jnp.int32, (16, w), 0)
        lead = lax.rem(lane, w // 2) // g - row
        for h in range(hh):
            vis = []
            for z in range(2):
                gap = 2 * (chip - src[h]) - z
                late = [jnp.where(gap + p >= 0, 0, 1) for p in range(2)]
                vis.append(lead >= jnp.where(lane < w // 2, late[0], late[1]))
            vt = kv[k, h, 1].T
            for a in range(nb):
                n = 16 * (a + 1)
                q = jnp.concatenate([qt[h, a, 0], qt[h, a, 1]], axis=1)
                s = []
                for z in range(2):
                    x = jnp.dot(kv[k, h, 0, z * t:z * t + n, :], q, preferred_element_type=jnp.float32)
                    edge = jnp.where(vis[z], x[n - 16:], NEG)
                    s.append(jnp.concatenate([x[:n - 16], edge], axis=0) if a else edge)
                old = m_ref[h, a]
                new = jnp.maximum(old, jnp.max(jnp.maximum(s[0], s[1]), axis=0, keepdims=True))
                m_ref[h, a] = new
                fade = jnp.exp2((old - new) * c)
                top = new * c
                e = [jnp.exp2(x * c - top) for x in s]
                l_ref[h, a] = l_ref[h, a] * fade + jnp.sum((e[0] + e[1]).reshape(n // 8, 8, w), axis=0)
                parts = []
                for x in e:
                    parts.append(x.astype(jnp.bfloat16))
                    if n < t:
                        parts.append(jnp.zeros((t - n, w), jnp.bfloat16))
                pv = jnp.dot(vt, jnp.concatenate(parts, axis=0), preferred_element_type=jnp.float32)
                acc[h, a] = acc[h, a] * fade + pv
        return carry

    lax.fori_loop(0, SLOTS + 1, step, 0)

    def out(h):
        mine = pltpu.make_async_copy(ost.at[iz, h], o_hbm.at[:, hh * iz + h], out_sem.at[0, h])
        theirs = remote(ost.at[oz, h], o_hbm.at[:, hh * iz + h], out_sem.at[1, h], out_sem.at[2, h], {"cz": oz})
        return mine, theirs

    @pl.loop(0, hh)
    def _(h):
        for a in range(nb):
            o = acc[h, a] * (1.0 / jnp.sum(l_ref[h, a], axis=0, keepdims=True))
            for p in range(2):
                x = o[:, p * 16 * g:(p + 1) * 16 * g].T
                ost[p, h, 16 * a:16 * (a + 1)] = x.reshape(16, g, d).astype(jnp.bfloat16)
        mine, theirs = out(h)
        theirs.start()
        mine.start()

    for slot in range(SLOTS):
        for n in range(4):
            unit(n, slot).wait_send()
            if slot < 2:
                rest(n, slot).wait_send()
    swap.wait_send()
    q_swap.wait_send()
    for h in range(hh):
        mine, theirs = out(h)
        mine.wait()
        theirs.wait_send()
        remote(ost.at[oz, h], o_hbm.at[:, hh * oz + h], out_sem.at[1, h], out_sem.at[2, h], {"cz": oz}).wait_recv()


def solution(mesh):
    assert mesh.shape["cx"] == RING and mesh.shape["cy"] == RING and mesh.shape["cz"] == 2
    spec = P(("dp", "cx", "cy", "cz"))

    def local(q, k, v):
        t, hq, d = q.shape
        hkv = k.shape[1]
        g = hq // hkv
        hh = hkv // 2
        nb = t // 16
        w = 2 * 16 * g
        units = SLOTS + 1
        o = pl.pallas_call(
            _kernel,
            out_shape=jax.ShapeDtypeStruct((t, hkv, g, d), jnp.bfloat16),
            in_specs=[pl.BlockSpec(memory_space=pl.ANY)] * 3,
            out_specs=pl.BlockSpec(memory_space=pl.ANY),
            scratch_shapes=[
                pltpu.VMEM((t, hkv, d), jnp.bfloat16),
                pltpu.VMEM((t, hkv, d), jnp.bfloat16),
                pltpu.VMEM((hkv, 2, t, d), jnp.bfloat16),
                pltpu.VMEM((units, hh, 2, 2 * t, d), jnp.bfloat16),
                pltpu.VMEM((2, t, hh, g, d), jnp.bfloat16),
                pltpu.VMEM((hh, nb, 2, d, 16 * g), jnp.bfloat16),
                pltpu.VMEM((hh, nb, d, w), jnp.float32),
                pltpu.VMEM((hh, nb, 1, w), jnp.float32),
                pltpu.VMEM((hh, nb, 8, w), jnp.float32),
                pltpu.VMEM((2, hh, t, g, d), jnp.bfloat16),
                pltpu.SMEM((hh,), jnp.int32),
                pltpu.SemaphoreType.DMA((3,)),
                pltpu.SemaphoreType.DMA((4,)),
                pltpu.SemaphoreType.DMA((4, SLOTS + 2)),
                pltpu.SemaphoreType.DMA((4, SLOTS + 2)),
                pltpu.SemaphoreType.DMA((3, hh)),
            ],
            compiler_params=pltpu.CompilerParams(collective_id=0, has_side_effects=True),
        )(k, v, q.reshape(t, hkv, g, d))
        return o.reshape(t, hq, d)

    return jax.shard_map(local, mesh=mesh, in_specs=(spec, spec, spec), out_specs=spec, check_vma=False)
```

time: 306 us -> 37.5 us (0.12)
  waiting for transfers between devices: 231 us -> 0 us
  Pallas kernels: 0 us -> 35.1 us
  other arithmetic: 26.2 us -> 0 us
  matrix products: 21.2 us -> 0 us
  between operations: 13.7 us -> 0.01 us
  local copies, waits for them, and re-layouts: 13.1 us -> 2.26 us
    all_gather x3 -> x0, waiting for transfers between devices: 88.5 us -> none  [the longest x1 44.5 us: local(): qg = lax.all_gather(q, 'cx', axis=0, tiled=True)]
    reduce_scatter x1 -> x0, waiting for transfers between devices: 80.3 us -> none  [local(): lax.psum_scatter(o, 'cx', scatter_dimension=0, tiled=True)]
    pallas_call x0 -> x1, Pallas kernels: none -> 35.1 us  [local(): pl.pallas_call(_kernel, out_shape=jax.ShapeDtypeStruct((t, hkv, g, d), jn...]
    pmax x1 -> x0, waiting for transfers between devices: 31.5 us -> none  [local(): top = lax.pmax(lse, 'cx')]
    psum x1 -> x0, waiting for transfers between devices: 28.7 us -> none  [local(): tot = top + jnp.log(lax.psum(jnp.exp(lse - top), 'cx'))]
    dot_general x8 -> x0, matrix products: 21.2 us -> none  [the longest x4 14.7 us: _partial(): jnp.einsum('haqgk,khd->aqhgd', p.astype(jnp.bfloat16), v[:e], preferred_e...]
    mul x3 -> x0, other arithmetic: 7.9 us -> none  [the longest x1 7.89 us: local(): o = o * jnp.exp(lse - tot)[..., None]]
    reduce_sum x4 -> x0, other arithmetic: 7.72 us -> none  [_partial(): l = jnp.transpose(jnp.sum(p, axis=-1), (1, 2, 0, 3))]
  transfers between devices with their start and end apart: 6 -> 0, of which waited for: 6 -> 0; matrix products, arithmetic and copies ran while one was open for 5% -> 0% of each run, Pallas kernels for 0% -> 0%
where the time goes in v1:
time: 37.5 us; the launch traced here: 37.4 us
  Pallas kernels  35.1 us (94%)
  local copies, waits for them, and re-layouts  2.26 us (6%)
    pallas_call x1, Pallas kernels, local(): pl.pallas_call(_kernel, out_shape=jax.ShapeDtypeStruct((t, hkv, g, d), jn...  35.1 us
    unnamed x1, local copies, waits for them, and re-layouts  2.26 us

profile of v1, /device:TPU:97, one launch (start us, length us, event | category | flops | bytes accessed | tf_op | source)
XLA Modules:
  0.0 37.4 jit_solution(3752657293178332618)
XLA Ops:
  0.0 35.1 %shard_map.37 = bf16[64,8,8,128]{3,2,1,0:T(8,128)(2,1)} custom-call(bf16[64,8,128]{2,1,0:T(8,128)(2,1)} %k_hbm.1, bf16[64,8,128]{2,1,0:T(8,128)(2,1)} %v_hbm.1, bf16[64,8,8,128]{3,2,1,0:T(8,128)(2,1)} %bitcast.3), custom_call_target="tpu_custom_call" | custom-call | tf_op jit(solution)/shard_map/pallas_call | solution.py:235
  35.1 2.3 %copy.5 = bf16[64,64,128]{2,1,0:T(8,128)(2,1)} copy(bf16[64,64,128]{2,1,0:T(8,128)(2,1)} %bitcast.2) | data formatting | bytes 2097152

commit v2 on v1

--- a/solution.py
+++ b/solution.py
@@ -44,7 +44,7 @@
 OFF = _offsets()
 
 
-def _kernel(k_hbm, v_hbm, q_hbm, o_hbm, kin, vin, st, kv, qs, qt, acc, m_ref, l_ref, ost, src,
+def _kernel(k_hbm, v_hbm, q_hbm, o_ref, kin, vin, st, kv, qs, qt, acc, m_ref, l_ref, ost, src,
             in_sem, x_sem, send_sem, recv_sem, out_sem):
     t, hkv, d = k_hbm.shape
     g = q_hbm.shape[2]
@@ -64,16 +64,16 @@
 
     half = lambda z: pl.ds(pl.multiple_of(z * t, t), t)
 
-    barrier = pltpu.get_barrier_semaphore()
-    for link in LINKS:
-        pl.semaphore_signal(barrier, inc=1, device_id=peer(link), device_id_type=pl.DeviceIdType.MESH)
-    pl.semaphore_signal(barrier, inc=1, device_id={"cz": oz}, device_id_type=pl.DeviceIdType.MESH)
     k_in = pltpu.make_async_copy(k_hbm, kin, in_sem.at[0])
     v_in = pltpu.make_async_copy(v_hbm, vin, in_sem.at[1])
     q_in = pltpu.make_async_copy(q_hbm.at[:, pl.ds(hh * iz, hh)], qs.at[iz], in_sem.at[2])
     k_in.start()
     v_in.start()
     q_in.start()
+    barrier = pltpu.get_barrier_semaphore()
+    for link in LINKS:
+        pl.semaphore_signal(barrier, inc=1, device_id=peer(link), device_id_type=pl.DeviceIdType.MESH)
+    pl.semaphore_signal(barrier, inc=1, device_id={"cz": oz}, device_id_type=pl.DeviceIdType.MESH)
 
     for n, (ref, copy) in enumerate(((kin, k_in), (vin, v_in))):
         copy.wait()
@@ -147,6 +147,11 @@
                     unit(n, j - 1).wait_recv()
                     if j - 1 < 2:
                         rest(n, j - 1).wait_recv()
+                for n in range(4):
+                    if j >= 2:
+                        unit(n, j - 2).wait_send()
+                    if 2 <= j < 4:
+                        rest(n, j - 2).wait_send()
                 if j - 1 + AHEAD < SLOTS:
                     for n in range(4):
                         unit(n, j - 1 + AHEAD).start()
@@ -188,36 +193,29 @@
                 acc[h, a] = acc[h, a] * fade + pv
         return carry
 
+    swap.wait_send()
+    q_swap.wait_send()
     lax.fori_loop(0, SLOTS + 1, step, 0)
 
     def out(h):
-        mine = pltpu.make_async_copy(ost.at[iz, h], o_hbm.at[:, hh * iz + h], out_sem.at[0, h])
-        theirs = remote(ost.at[oz, h], o_hbm.at[:, hh * iz + h], out_sem.at[1, h], out_sem.at[2, h], {"cz": oz})
-        return mine, theirs
+        return remote(ost.at[h], o_ref.at[:, hh * iz + h], out_sem.at[0, h], out_sem.at[1, h], {"cz": oz})
 
     @pl.loop(0, hh)
     def _(h):
         for a in range(nb):
             o = acc[h, a] * (1.0 / jnp.sum(l_ref[h, a], axis=0, keepdims=True))
-            for p in range(2):
-                x = o[:, p * 16 * g:(p + 1) * 16 * g].T
-                ost[p, h, 16 * a:16 * (a + 1)] = x.reshape(16, g, d).astype(jnp.bfloat16)
-        mine, theirs = out(h)
-        theirs.start()
-        mine.start()
-
-    for slot in range(SLOTS):
-        for n in range(4):
-            unit(n, slot).wait_send()
-            if slot < 2:
-                rest(n, slot).wait_send()
-    swap.wait_send()
-    q_swap.wait_send()
+            x = [o[:, p * 16 * g:(p + 1) * 16 * g].T.reshape(16, g, d).astype(jnp.bfloat16) for p in range(2)]
+            here = iz == 0
+            ost[h, 16 * a:16 * (a + 1)] = jnp.where(here, x[1], x[0])
+            o_ref[16 * a:16 * (a + 1), hh * iz + h] = jnp.where(here, x[0], x[1])
+        out(h).start()
+
+    for n in range(4):
+        unit(n, SLOTS - 1).wait_send()
     for h in range(hh):
-        mine, theirs = out(h)
-        mine.wait()
+        theirs = out(h)
         theirs.wait_send()
-        remote(ost.at[oz, h], o_hbm.at[:, hh * oz + h], out_sem.at[1, h], out_sem.at[2, h], {"cz": oz}).wait_recv()
+        theirs.wait_recv()
 
 
 def solution(mesh):
@@ -235,8 +233,8 @@
         o = pl.pallas_call(
             _kernel,
             out_shape=jax.ShapeDtypeStruct((t, hkv, g, d), jnp.bfloat16),
-            in_specs=[pl.BlockSpec(memory_space=pl.ANY)] * 3,
-            out_specs=pl.BlockSpec(memory_space=pl.ANY),
+            in_specs=[pl.BlockSpec(memory_space=pltpu.HBM)] * 3,
+            out_specs=pl.BlockSpec(memory_space=pltpu.VMEM),
             scratch_shapes=[
                 pltpu.VMEM((t, hkv, d), jnp.bfloat16),
                 pltpu.VMEM((t, hkv, d), jnp.bfloat16),
@@ -247,16 +245,16 @@
                 pltpu.VMEM((hh, nb, d, w), jnp.float32),
                 pltpu.VMEM((hh, nb, 1, w), jnp.float32),
                 pltpu.VMEM((hh, nb, 8, w), jnp.float32),
-                pltpu.VMEM((2, hh, t, g, d), jnp.bfloat16),
+                pltpu.VMEM((hh, t, g, d), jnp.bfloat16),
                 pltpu.SMEM((hh,), jnp.int32),
                 pltpu.SemaphoreType.DMA((3,)),
                 pltpu.SemaphoreType.DMA((4,)),
                 pltpu.SemaphoreType.DMA((4, SLOTS + 2)),
                 pltpu.SemaphoreType.DMA((4, SLOTS + 2)),
-                pltpu.SemaphoreType.DMA((3, hh)),
+                pltpu.SemaphoreType.DMA((2, hh)),
             ],
-            compiler_params=pltpu.CompilerParams(collective_id=0, has_side_effects=True),
-        )(k, v, q.reshape(t, hkv, g, d))
+            compiler_params=pltpu.CompilerParams(collective_id=0, has_side_effects=True, vmem_limit_bytes=20 << 20),
+        )(*(pltpu.with_memory_space_constraint(x, pltpu.HBM) for x in (k, v, q.reshape(t, hkv, g, d))))
         return o.reshape(t, hq, d)
 
     return jax.shard_map(local, mesh=mesh, in_specs=(spec, spec, spec), out_specs=spec, check_vma=False)

time: 37.5 us -> 36.2 us (0.965)
  local copies, waits for them, and re-layouts: 2.26 us -> 0.97 us
    unnamed x1, local copies, waits for them, and re-layouts: 2.26 us -> 0.97 us
where the time goes in v2:
time: 36.2 us; the launch traced here: 36.1 us
  Pallas kernels  35.1 us (97%)
  local copies, waits for them, and re-layouts  0.97 us (3%)
    pallas_call x1, Pallas kernels, local(): pl.pallas_call(_kernel, out_shape=jax.ShapeDtypeStruct((t, hkv, g, d), jn...  35.1 us
    unnamed x1, local copies, waits for them, and re-layouts  0.97 us

profile of v2, /device:TPU:97, one launch (start us, length us, event | category | flops | bytes accessed | tf_op | source)
XLA Modules:
  0.0 36.1 jit_solution(9994216601001376524)
XLA Ops:
  0.0 35.1 %shard_map.37 = bf16[64,8,8,128]{3,2,1,0:T(8,128)(2,1)S(1)} custom-call(bf16[64,8,128]{2,1,0:T(8,128)(2,1)} %k_hbm.1, bf16[64,8,128]{2,1,0:T(8,128)(2,1)} %v_hbm.1, bf16[64,8,8,128]{3,2,1,0:T(8,128)(2,1)} %bitcast.3), custom_call_target="tpu_custom_call" | custom-call | tf_op jit(solution)/shard_map/pallas_call | solution.py:233
  35.1 1.0 %copy.5 = bf16[64,64,128]{2,1,0:T(8,128)(2,1)} copy(bf16[64,64,128]{2,1,0:T(8,128)(2,1)S(1)} %bitcast.2) | data formatting | bytes 2097152

commit v3 on v2

v3 whole, which is shorter than its diff:
```python
import functools
import math

import jax
import jax.numpy as jnp
from jax import lax
from jax.experimental import pallas as pl
from jax.experimental.pallas import tpu as pltpu
from jax.sharding import PartitionSpec as P

NEG = -1e30
RING = 4
LINKS = (("x", 1), ("x", -1), ("y", 1), ("y", -1))
HEAD_OF = {("x", 1): 0, ("x", -1): 1, ("y", 1): 2, ("y", -1): 3}
PLAN = (
    ("a", -1), ("b", -1), ("c", -1), ("d", -1), ("a", 0), ("c", 0), ("c", 1), ("d", 1),
    ("c", 4), ("c", 2), ("c", 5), ("c", 6), ("d", 0), ("c", 8), ("d", 4),
)
SLOTS = len(PLAN)
AHEAD = 4
WHOLE = 11


def _head(link, letter):
    axis, sign = link
    other = "y" if axis == "x" else "x"
    return HEAD_OF[{"a": (axis, sign), "b": (axis, -sign), "c": (other, sign), "d": (other, -sign)}[letter]]


def _offsets():
    off = [dict() for _ in range(SLOTS)]
    for slot, (letter, src) in enumerate(PLAN):
        for link in LINKS:
            head = _head(link, letter)
            x, y = (0, 0) if src < 0 else off[src][head]
            axis, sign = link
            x, y = (x + sign, y) if axis == "x" else (x, y + sign)
            assert head not in off[slot]
            off[slot][head] = (x % RING, y % RING)
    for head in range(len(LINKS)):
        assert len({off[s][head] for s in range(SLOTS)} | {(0, 0)}) == RING * RING
    return off


OFF = _offsets()


def _kernel(k_hbm, v_hbm, q_hbm, o_ref, kin, vin, st, kv, qs, qt, acc, m_ref, l_ref, ost, sc, src,
            in_sem, x_sem, send_sem, recv_sem, out_sem):
    t, hkv, d = k_hbm.shape
    g = q_hbm.shape[2]
    hh = hkv // 2
    nb = t // 16
    w = 2 * 16 * g
    iy, ix, iz = lax.axis_index("cx"), lax.axis_index("cy"), lax.axis_index("cz")
    oz = 1 - iz
    chip = iy * RING + ix
    c = d ** -0.5 * math.log2(math.e)

    def peer(link):
        axis, sign = link
        if axis == "x":
            return {"cy": lax.rem(ix + sign + RING, RING)}
        return {"cx": lax.rem(iy + sign + RING, RING)}

    low, high = slice(0, t // 2), slice(t // 2, t)

    k_in = pltpu.make_async_copy(k_hbm, kin, in_sem.at[0])
    v_in = pltpu.make_async_copy(v_hbm, vin, in_sem.at[1])
    q_in = pltpu.make_async_copy(q_hbm.at[:, pl.ds(hh * iz, hh)], qs.at[iz], in_sem.at[2])
    k_in.start()
    v_in.start()
    q_in.start()
    barrier = pltpu.get_barrier_semaphore()
    for link in LINKS:
        pl.semaphore_signal(barrier, inc=1, device_id=peer(link), device_id_type=pl.DeviceIdType.MESH)
    pl.semaphore_signal(barrier, inc=1, device_id={"cz": oz}, device_id_type=pl.DeviceIdType.MESH)

    for n, (ref, copy) in enumerate(((kin, k_in), (vin, v_in))):
        copy.wait()
        x = jnp.swapaxes(ref[...].astype(jnp.float32), 0, 1)
        st[:, n] = x.astype(jnp.bfloat16)
    for h in range(hh):
        kv[0, h, :, iz] = st[hh * iz + h]

    def remote(a, b, s, r, to):
        return pltpu.make_async_remote_copy(
            src_ref=a, dst_ref=b, send_sem=s, recv_sem=r, device_id=to, device_id_type=pl.DeviceIdType.MESH)

    def unit(n, slot, part=0):
        link = LINKS[n]
        letter, arrival = PLAN[slot]
        h = _head(link, letter)
        here, there = kv.at[1 + arrival, h], kv.at[1 + slot, h]
        if slot < 2:
            z = (iz, oz)[part]
            here, there = (kv.at[0, h, :, z] if part else st.at[hh * iz + h]), there.at[:, z]
        elif slot >= WHOLE:
            rows = (low, high)[part]
            here, there = here.at[:, :, rows], there.at[:, :, rows]
        return remote(here, there, send_sem.at[part, n, slot], recv_sem.at[part, n, slot], peer(link))

    def parts(slot):
        return (0, 1) if slot < 2 or slot >= WHOLE else (0,)

    swap = remote(st.at[pl.ds(hh * oz, hh)], kv.at[0, :, :, iz], x_sem.at[0], x_sem.at[1], {"cz": oz})
    q_swap = remote(q_hbm.at[:, pl.ds(hh * oz, hh)], qs.at[iz], x_sem.at[2], x_sem.at[3], {"cz": oz})

    pl.semaphore_wait(barrier, len(LINKS) + 1)
    swap.start()
    for slot in range(2):
        for n in range(4):
            unit(n, slot).start()
    q_swap.start()
    swap.wait_recv()
    for slot in range(2):
        for n in range(4):
            unit(n, slot, 1).start()
    for slot in range(2, AHEAD):
        for n in range(4):
            unit(n, slot).start()

    m_ref[...] = jnp.full_like(m_ref, NEG)
    l_ref[...] = jnp.zeros_like(l_ref)
    acc[...] = jnp.zeros_like(acc)

    def turn(p):
        @pl.loop(0, hh)
        def _(h):
            for a in range(nb):
                x = qs[p, 16 * a:16 * (a + 1), h].astype(jnp.float32).reshape(16 * g, d)
                qt[h, a, p] = x.T.astype(jnp.bfloat16)

    q_in.wait()
    q_swap.wait_recv()
    for p in range(2):
        turn(p)

    def origin(slot):
        for h in range(hh):
            ox, oy = OFF[slot][h]
            src[slot + 1, h] = lax.rem(iy - oy + RING, RING) * RING + lax.rem(ix - ox + RING, RING)

    lane = lax.broadcasted_iota(jnp.int32, (16, w), 1)
    row = lax.broadcasted_iota(jnp.int32, (16, w), 0)
    lead = lax.rem(lane, w // 2) // g - row

    def attend(k, r0, r1):
        first = r0 // 16

        def scores(h, a):
            n = min(r1, 16 * (a + 1)) - r0
            q = jnp.concatenate([qt[h, a, 0], qt[h, a, 1]], axis=1)
            keys = jnp.concatenate([kv[k, h, 0, z, r0:r0 + n] for z in range(2)], axis=0)
            sc[h % 2, a, :2 * n] = jnp.dot(keys, q, preferred_element_type=jnp.float32)

        def weigh(h):
            vis = []
            for z in range(2):
                gap = 2 * (chip - src[k, h]) - z
                late = [jnp.where(gap + p >= 0, 0, 1) for p in range(2)]
                vis.append(lead >= jnp.where(lane < w // 2, late[0], late[1]))
            vt = kv[k, h, 1, :, r0:r1].reshape(2 * (r1 - r0), d).T
            for a in range(first, nb):
                n = min(r1, 16 * (a + 1)) - r0
                s = []
                for z in range(2):
                    x = sc[h % 2, a, z * n:(z + 1) * n]
                    if 16 * (a + 1) <= r1:
                        edge = jnp.where(vis[z], x[n - 16:], NEG)
                        x = jnp.concatenate([x[:n - 16], edge], axis=0) if n > 16 else edge
                    s.append(x)
                old = m_ref[h, a]
                new = jnp.maximum(old, jnp.max(jnp.maximum(s[0], s[1]), axis=0, keepdims=True))
                m_ref[h, a] = new
                fade = jnp.exp2((old - new) * c)
                top = new * c
                e = [jnp.exp2(x * c - top) for x in s]
                l_ref[h, a] = l_ref[h, a] * fade + jnp.sum((e[0] + e[1]).reshape(n // 8, 8, w), axis=0)
                weights = []
                for x in e:
                    weights.append(x.astype(jnp.bfloat16))
                    if n < r1 - r0:
                        weights.append(jnp.zeros((r1 - r0 - n, w), jnp.bfloat16))
                pv = jnp.dot(vt, jnp.concatenate(weights, axis=0), preferred_element_type=jnp.float32)
                acc[h, a] = acc[h, a] * fade + pv

        for a in range(first, nb):
            scores(0, a)
        for h in range(hh):
            if h + 1 < hh:
                for a in range(first, nb):
                    scores(h + 1, a)
            weigh(h)

    def finish(a0, a1):
        for h in range(hh):
            for a in range(a0, a1):
                o = acc[h, a] * (1.0 / jnp.sum(l_ref[h, a], axis=0, keepdims=True))
                x = [o[:, p * 16 * g:(p + 1) * 16 * g].T.reshape(16, g, d).astype(jnp.bfloat16) for p in range(2)]
                here = iz == 0
                ost[16 * a:16 * (a + 1), h] = jnp.where(here, x[1], x[0])
                o_ref[16 * a:16 * (a + 1), hh * iz + h] = jnp.where(here, x[0], x[1])

    def out(n):
        rows = (low, high)[n]
        return remote(ost.at[rows], o_ref.at[rows, pl.ds(hh * iz, hh)], out_sem.at[0, n], out_sem.at[1, n], {"cz": oz})

    tail = [(part, slot) for part in range(2) for slot in range(WHOLE, SLOTS)]
    first = WHOLE - AHEAD + 1
    late = {first: tail[:2], first + 1: tail[2:5], first + 2: tail[5:]}

    def whole(k, carry):
        for j in range(1, WHOLE + 1):
            @pl.when(k == j)
            def _():
                for n in range(4):
                    for part in parts(j - 1):
                        unit(n, j - 1, part).wait_recv()
                for n in range(4):
                    if j >= 2:
                        for part in parts(j - 2):
                            unit(n, j - 2, part).wait_send()
                if j - 1 + AHEAD < WHOLE:
                    for n in range(4):
                        unit(n, j - 1 + AHEAD).start()
                for part, slot in late.get(j, ()):
                    for n in range(4):
                        unit(n, slot, part).start()
        attend(k, 0, t)
        return carry

    def lows(k, carry):
        for n in range(4):
            land(n, k - 1, 0).wait_recv()
        attend(k, 0, t // 2)
        return carry

    def highs(k, carry):
        for n in range(4):
            land(n, k - 1, 1).wait_recv()
        attend(k, t // 2, t)
        return carry

    def land(n, slot, part):
        piece = kv.at[1 + slot, n].at[:, :, (low, high)[part]]
        return remote(piece, piece, send_sem.at[part, n, slot], recv_sem.at[part, n, slot], peer(LINKS[n]))

    for h in range(hh):
        src[0, h] = chip
    for slot in range(SLOTS):
        origin(slot)
    swap.wait_send()
    q_swap.wait_send()
    lax.fori_loop(0, WHOLE + 1, whole, 0)
    lax.fori_loop(WHOLE + 1, SLOTS + 1, lows, 0)
    finish(0, nb // 2)
    out(0).start()
    lax.fori_loop(WHOLE + 1, SLOTS + 1, highs, 0)
    finish(nb // 2, nb)
    out(1).start()
    for n in range(4):
        unit(n, WHOLE - 1).wait_send()
        for slot in range(WHOLE, SLOTS):
            for part in range(2):
                unit(n, slot, part).wait_send()
    for n in range(2):
        out(n).wait_send()
        out(n).wait_recv()


def solution(mesh):
    assert mesh.shape["cx"] == RING and mesh.shape["cy"] == RING and mesh.shape["cz"] == 2
    spec = P(("dp", "cx", "cy", "cz"))

    def local(q, k, v):
        t, hq, d = q.shape
        hkv = k.shape[1]
        g = hq // hkv
        hh = hkv // 2
        nb = t // 16
        w = 2 * 16 * g
        units = SLOTS + 1
        o = pl.pallas_call(
            _kernel,
            out_shape=jax.ShapeDtypeStruct((t, hkv, g, d), jnp.bfloat16),
            in_specs=[pl.BlockSpec(memory_space=pltpu.HBM)] * 3,
            out_specs=pl.BlockSpec(memory_space=pltpu.VMEM),
            scratch_shapes=[
                pltpu.VMEM((t, hkv, d), jnp.bfloat16),
                pltpu.VMEM((t, hkv, d), jnp.bfloat16),
                pltpu.VMEM((hkv, 2, t, d), jnp.bfloat16),
                pltpu.VMEM((units, hh, 2, 2, t, d), jnp.bfloat16),
                pltpu.VMEM((2, t, hh, g, d), jnp.bfloat16),
                pltpu.VMEM((hh, nb, 2, d, 16 * g), jnp.bfloat16),
                pltpu.VMEM((hh, nb, d, w), jnp.float32),
                pltpu.VMEM((hh, nb, 1, w), jnp.float32),
                pltpu.VMEM((hh, nb, 8, w), jnp.float32),
                pltpu.VMEM((t, hh, g, d), jnp.bfloat16),
                pltpu.VMEM((2, nb, 2 * t, w), jnp.float32),
                pltpu.SMEM((units, hh), jnp.int32),
                pltpu.SemaphoreType.DMA((3,)),
                pltpu.SemaphoreType.DMA((4,)),
                pltpu.SemaphoreType.DMA((2, 4, SLOTS)),
                pltpu.SemaphoreType.DMA((2, 4, SLOTS)),
                pltpu.SemaphoreType.DMA((2, 2)),
            ],
            compiler_params=pltpu.CompilerParams(collective_id=0, has_side_effects=True, vmem_limit_bytes=20 << 20),
        )(*(pltpu.with_memory_space_constraint(x, pltpu.HBM) for x in (k, v, q.reshape(t, hkv, g, d))))
        return o.reshape(t, hq, d)

    return jax.shard_map(local, mesh=mesh, in_specs=(spec, spec, spec), out_specs=spec, check_vma=False)
```

time: 36.2 us -> 36.6 us (1.011)
  Pallas kernels: 35.1 us -> 35.6 us
    pallas_call x1, Pallas kernels: 35.1 us -> 35.6 us  [local(): pl.pallas_call(_kernel, out_shape=jax.ShapeDtypeStruct((t, hkv, g, d), jn...]
where the time goes in v3:
time: 36.6 us
  Pallas kernels  35.6 us (97%)
  local copies, waits for them, and re-layouts  0.97 us (3%)
    pallas_call x1, Pallas kernels, local(): pl.pallas_call(_kernel, out_shape=jax.ShapeDtypeStruct((t, hkv, g, d), jn...  35.6 us
    unnamed x1, local copies, waits for them, and re-layouts  0.97 us

profile of v3, /device:TPU:97, one launch (start us, length us, event | category | flops | bytes accessed | tf_op | source)
XLA Modules:
  0.0 36.6 jit_solution(14273741909260111658)
XLA Ops:
  0.0 35.6 %shard_map.37 = bf16[64,8,8,128]{3,2,1,0:T(8,128)(2,1)S(1)} custom-call(bf16[64,8,128]{2,1,0:T(8,128)(2,1)} %k_hbm.1, bf16[64,8,128]{2,1,0:T(8,128)(2,1)} %v_hbm.1, bf16[64,8,8,128]{3,2,1,0:T(8,128)(2,1)} %bitcast.3), custom_call_target="tpu_custom_call" | custom-call | tf_op jit(solution)/shard_map/pallas_call | solution.py:284
  35.6 1.0 %copy.5 = bf16[64,64,128]{2,1,0:T(8,128)(2,1)} copy(bf16[64,64,128]{2,1,0:T(8,128)(2,1)S(1)} %bitcast.2) | data formatting | bytes 2097152

commit v4 on v2

--- a/solution.py
+++ b/solution.py
@@ -44,7 +44,7 @@
 OFF = _offsets()
 
 
-def _kernel(k_hbm, v_hbm, q_hbm, o_ref, kin, vin, st, kv, qs, qt, acc, m_ref, l_ref, ost, src,
+def _kernel(k_hbm, v_hbm, q_hbm, o_ref, kin, vin, st, kv, qs, qt, acc, m_ref, l_ref, ost, sc, src,
             in_sem, x_sem, send_sem, recv_sem, out_sem):
     t, hkv, d = k_hbm.shape
     g = q_hbm.shape[2]
@@ -162,7 +162,13 @@
         lane = lax.broadcasted_iota(jnp.int32, (16, w), 1)
         row = lax.broadcasted_iota(jnp.int32, (16, w), 0)
         lead = lax.rem(lane, w // 2) // g - row
-        for h in range(hh):
+        def scores(h, a):
+            n = 16 * (a + 1)
+            q = jnp.concatenate([qt[h, a, 0], qt[h, a, 1]], axis=1)
+            keys = jnp.concatenate([kv[k, h, 0, z * t:z * t + n, :] for z in range(2)], axis=0)
+            sc[h % 2, a, :2 * n] = jnp.dot(keys, q, preferred_element_type=jnp.float32)
+
+        def weigh(h):
             vis = []
             for z in range(2):
                 gap = 2 * (chip - src[h]) - z
@@ -171,12 +177,10 @@
             vt = kv[k, h, 1].T
             for a in range(nb):
                 n = 16 * (a + 1)
-                q = jnp.concatenate([qt[h, a, 0], qt[h, a, 1]], axis=1)
                 s = []
                 for z in range(2):
-                    x = jnp.dot(kv[k, h, 0, z * t:z * t + n, :], q, preferred_element_type=jnp.float32)
-                    edge = jnp.where(vis[z], x[n - 16:], NEG)
-                    s.append(jnp.concatenate([x[:n - 16], edge], axis=0) if a else edge)
+                    edge = jnp.where(vis[z], sc[h % 2, a, (z + 1) * n - 16:(z + 1) * n], NEG)
+                    s.append(jnp.concatenate([sc[h % 2, a, z * n:(z + 1) * n - 16], edge], axis=0) if a else edge)
                 old = m_ref[h, a]
                 new = jnp.maximum(old, jnp.max(jnp.maximum(s[0], s[1]), axis=0, keepdims=True))
                 m_ref[h, a] = new
@@ -191,6 +195,14 @@
                         parts.append(jnp.zeros((t - n, w), jnp.bfloat16))
                 pv = jnp.dot(vt, jnp.concatenate(parts, axis=0), preferred_element_type=jnp.float32)
                 acc[h, a] = acc[h, a] * fade + pv
+
+        for a in range(nb):
+            scores(0, a)
+        for h in range(hh):
+            if h + 1 < hh:
+                for a in range(nb):
+                    scores(h + 1, a)
+            weigh(h)
         return carry
 
     swap.wait_send()
@@ -246,6 +258,7 @@
                 pltpu.VMEM((hh, nb, 1, w), jnp.float32),
                 pltpu.VMEM((hh, nb, 8, w), jnp.float32),
                 pltpu.VMEM((hh, t, g, d), jnp.bfloat16),
+                pltpu.VMEM((2, nb, 2 * t, w), jnp.float32),
                 pltpu.SMEM((hh,), jnp.int32),
                 pltpu.SemaphoreType.DMA((3,)),
                 pltpu.SemaphoreType.DMA((4,)),

time: 36.2 us -> 35.9 us (level)
  no operation moved by 1% of the time
where the time goes in v4:
time: 35.9 us; the launch traced here: 35.8 us
  Pallas kernels  34.9 us (97%)
  local copies, waits for them, and re-layouts  0.97 us (3%)
    pallas_call x1, Pallas kernels, local(): pl.pallas_call(_kernel, out_shape=jax.ShapeDtypeStruct((t, hkv, g, d), jn...  34.9 us
    unnamed x1, local copies, waits for them, and re-layouts  0.97 us

profile of v4, /device:TPU:97, one launch (start us, length us, event | category | flops | bytes accessed | tf_op | source)
XLA Modules:
  0.0 35.8 jit_solution(5308384438296985159)
XLA Ops:
  0.0 34.9 %shard_map.37 = bf16[64,8,8,128]{3,2,1,0:T(8,128)(2,1)S(1)} custom-call(bf16[64,8,128]{2,1,0:T(8,128)(2,1)} %k_hbm.1, bf16[64,8,128]{2,1,0:T(8,128)(2,1)} %v_hbm.1, bf16[64,8,8,128]{3,2,1,0:T(8,128)(2,1)} %bitcast.3), custom_call_target="tpu_custom_call" | custom-call | tf_op jit(solution)/shard_map/pallas_call | solution.py:245
  34.9 1.0 %copy.5 = bf16[64,64,128]{2,1,0:T(8,128)(2,1)} copy(bf16[64,64,128]{2,1,0:T(8,128)(2,1)S(1)} %bitcast.2) | data formatting | bytes 2097152

commit v5 on v4

--- a/solution.py
+++ b/solution.py
@@ -90,16 +90,19 @@
         link = LINKS[n]
         letter, arrival = PLAN[slot]
         h = _head(link, letter)
-        sems = send_sem.at[n, slot], recv_sem.at[n, slot], peer(link)
+        sems = send_sem.at[0], recv_sem.at[slot], peer(link)
         if slot < 2:
             return remote(st.at[hh * iz + h], kv.at[1 + slot, h, :, half(iz), :], *sems)
         return remote(kv.at[1 + arrival, h], kv.at[1 + slot, h], *sems)
+
+    def landed(ref, sem):
+        pltpu.make_async_copy(ref, ref, sem).wait()
 
     def rest(n, slot):
         link = LINKS[n]
         h = _head(link, PLAN[slot][0])
         return remote(kv.at[0, h, :, half(oz), :], kv.at[1 + slot, h, :, half(oz), :],
-                      send_sem.at[n, SLOTS + slot], recv_sem.at[n, SLOTS + slot], peer(link))
+                      send_sem.at[0], recv_sem.at[slot], peer(link))
 
     swap = remote(st.at[pl.ds(hh * oz, hh)], kv.at[0, :, :, half(iz), :], x_sem.at[0], x_sem.at[1], {"cz": oz})
     q_swap = remote(q_hbm.at[:, pl.ds(hh * oz, hh)], qs.at[iz], x_sem.at[2], x_sem.at[3], {"cz": oz})
@@ -143,15 +146,7 @@
         for j in range(1, SLOTS + 1):
             @pl.when(k == j)
             def _():
-                for n in range(4):
-                    unit(n, j - 1).wait_recv()
-                    if j - 1 < 2:
-                        rest(n, j - 1).wait_recv()
-                for n in range(4):
-                    if j >= 2:
-                        unit(n, j - 2).wait_send()
-                    if 2 <= j < 4:
-                        rest(n, j - 2).wait_send()
+                landed(kv.at[j], recv_sem.at[j - 1])
                 if j - 1 + AHEAD < SLOTS:
                     for n in range(4):
                         unit(n, j - 1 + AHEAD).start()
@@ -210,24 +205,22 @@
     lax.fori_loop(0, SLOTS + 1, step, 0)
 
     def out(h):
-        return remote(ost.at[h], o_ref.at[:, hh * iz + h], out_sem.at[0, h], out_sem.at[1, h], {"cz": oz})
+        return remote(ost.at[h], o_ref.at[:, hh * iz + h], out_sem.at[0], out_sem.at[1], {"cz": oz})
 
     @pl.loop(0, hh)
     def _(h):
         for a in range(nb):
             o = acc[h, a] * (1.0 / jnp.sum(l_ref[h, a], axis=0, keepdims=True))
-            x = [o[:, p * 16 * g:(p + 1) * 16 * g].T.reshape(16, g, d).astype(jnp.bfloat16) for p in range(2)]
+            o = o.astype(jnp.bfloat16)
+            x = [o[:, p * 16 * g:(p + 1) * 16 * g].T.reshape(16, g, d) for p in range(2)]
             here = iz == 0
             ost[h, 16 * a:16 * (a + 1)] = jnp.where(here, x[1], x[0])
             o_ref[16 * a:16 * (a + 1), hh * iz + h] = jnp.where(here, x[0], x[1])
         out(h).start()
 
-    for n in range(4):
-        unit(n, SLOTS - 1).wait_send()
-    for h in range(hh):
-        theirs = out(h)
-        theirs.wait_send()
-        theirs.wait_recv()
+    landed(kv.at[pl.ds(1, SLOTS)], send_sem.at[0])
+    landed(ost, out_sem.at[0])
+    landed(o_ref.at[:, pl.ds(hh * oz, hh)], out_sem.at[1])
 
 
 def solution(mesh):
@@ -262,9 +255,9 @@
                 pltpu.SMEM((hh,), jnp.int32),
                 pltpu.SemaphoreType.DMA((3,)),
                 pltpu.SemaphoreType.DMA((4,)),
-                pltpu.SemaphoreType.DMA((4, SLOTS + 2)),
-                pltpu.SemaphoreType.DMA((4, SLOTS + 2)),
-                pltpu.SemaphoreType.DMA((2, hh)),
+                pltpu.SemaphoreType.DMA((1,)),
+                pltpu.SemaphoreType.DMA((SLOTS,)),
+                pltpu.SemaphoreType.DMA((2,)),
             ],
             compiler_params=pltpu.CompilerParams(collective_id=0, has_side_effects=True, vmem_limit_bytes=20 << 20),
         )(*(pltpu.with_memory_space_constraint(x, pltpu.HBM) for x in (k, v, q.reshape(t, hkv, g, d))))

time: 35.9 us -> 34.8 us (0.969)
  Pallas kernels: 34.9 us -> 33.7 us
    pallas_call x1, Pallas kernels: 34.9 us -> 33.7 us  [local(): pl.pallas_call(_kernel, out_shape=jax.ShapeDtypeStruct((t, hkv, g, d), jn...]
where the time goes in v5:
time: 34.8 us; the launch traced here: 34.7 us
  Pallas kernels  33.7 us (97%)
  local copies, waits for them, and re-layouts  0.97 us (3%)
    pallas_call x1, Pallas kernels, local(): pl.pallas_call(_kernel, out_shape=jax.ShapeDtypeStruct((t, hkv, g, d), jn...  33.7 us
    unnamed x1, local copies, waits for them, and re-layouts  0.97 us

profile of v5, /device:TPU:97, one launch (start us, length us, event | category | flops | bytes accessed | tf_op | source)
XLA Modules:
  0.0 34.7 jit_solution(16900615136792742743)
XLA Ops:
  0.0 33.7 %shard_map.37 = bf16[64,8,8,128]{3,2,1,0:T(8,128)(2,1)S(1)} custom-call(bf16[64,8,128]{2,1,0:T(8,128)(2,1)} %k_hbm.1, bf16[64,8,128]{2,1,0:T(8,128)(2,1)} %v_hbm.1, bf16[64,8,8,128]{3,2,1,0:T(8,128)(2,1)} %bitcast.3), custom_call_target="tpu_custom_call" | custom-call | tf_op jit(solution)/shard_map/pallas_call | solution.py:238
  33.7 1.0 %copy.5 = bf16[64,64,128]{2,1,0:T(8,128)(2,1)} copy(bf16[64,64,128]{2,1,0:T(8,128)(2,1)S(1)} %bitcast.2) | data formatting | bytes 2097152

commit v6 on v5

--- a/solution.py
+++ b/solution.py
@@ -18,6 +18,7 @@
 )
 SLOTS = len(PLAN)
 AHEAD = 4
+LAG = 2
 
 
 def _head(link, letter):
@@ -147,9 +148,19 @@
             @pl.when(k == j)
             def _():
                 landed(kv.at[j], recv_sem.at[j - 1])
-                if j - 1 + AHEAD < SLOTS:
+                if j - 1 + AHEAD < SLOTS - 1:
                     for n in range(4):
                         unit(n, j - 1 + AHEAD).start()
+                if j - 1 + AHEAD == SLOTS - 1:
+                    @pl.when(iz == 0)
+                    def _():
+                        for n in range(4):
+                            unit(n, SLOTS - 1).start()
+                if j == SLOTS - LAG:
+                    @pl.when(iz == 1)
+                    def _():
+                        for n in range(4):
+                            unit(n, SLOTS - 1).start()
                 for h in range(hh):
                     ox, oy = OFF[j - 1][h]
                     src[h] = lax.rem(iy - oy + RING, RING) * RING + lax.rem(ix - ox + RING, RING)

time: 34.8 us -> 34.4 us (0.989)
  Pallas kernels: 33.7 us -> 33.3 us
    pallas_call x1, Pallas kernels: 33.7 us -> 33.3 us  [local(): pl.pallas_call(_kernel, out_shape=jax.ShapeDtypeStruct((t, hkv, g, d), jn...]
where the time goes in v6:
time: 34.4 us; the launch traced here: 34.3 us
  Pallas kernels  33.3 us (97%)
  local copies, waits for them, and re-layouts  0.97 us (3%)
    pallas_call x1, Pallas kernels, local(): pl.pallas_call(_kernel, out_shape=jax.ShapeDtypeStruct((t, hkv, g, d), jn...  33.3 us
    unnamed x1, local copies, waits for them, and re-layouts  0.97 us

profile of v6, /device:TPU:97, one launch (start us, length us, event | category | flops | bytes accessed | tf_op | source)
XLA Modules:
  0.0 34.3 jit_solution(10361751481372506457)
XLA Ops:
  0.0 33.3 %shard_map.37 = bf16[64,8,8,128]{3,2,1,0:T(8,128)(2,1)S(1)} custom-call(bf16[64,8,128]{2,1,0:T(8,128)(2,1)} %k_hbm.1, bf16[64,8,128]{2,1,0:T(8,128)(2,1)} %v_hbm.1, bf16[64,8,8,128]{3,2,1,0:T(8,128)(2,1)} %bitcast.3), custom_call_target="tpu_custom_call" | custom-call | tf_op jit(solution)/shard_map/pallas_call | solution.py:249
  33.3 1.0 %copy.5 = bf16[64,64,128]{2,1,0:T(8,128)(2,1)} copy(bf16[64,64,128]{2,1,0:T(8,128)(2,1)S(1)} %bitcast.2) | data formatting | bytes 2097152

commit v7 on v3

--- a/solution.py
+++ b/solution.py
@@ -18,7 +18,8 @@
 )
 SLOTS = len(PLAN)
 AHEAD = 4
-WHOLE = 11
+WHOLE = SLOTS - 2
+LAG = 2
 
 
 def _head(link, letter):
@@ -91,17 +92,17 @@
         link = LINKS[n]
         letter, arrival = PLAN[slot]
         h = _head(link, letter)
-        here, there = kv.at[1 + arrival, h], kv.at[1 + slot, h]
+        here, there, to = kv.at[1 + arrival, h], kv.at[1 + slot, h], slot
         if slot < 2:
             z = (iz, oz)[part]
             here, there = (kv.at[0, h, :, z] if part else st.at[hh * iz + h]), there.at[:, z]
         elif slot >= WHOLE:
-            rows = (low, high)[part]
+            rows, to = (low, high)[part], WHOLE + part
             here, there = here.at[:, :, rows], there.at[:, :, rows]
-        return remote(here, there, send_sem.at[part, n, slot], recv_sem.at[part, n, slot], peer(link))
-
-    def parts(slot):
-        return (0, 1) if slot < 2 or slot >= WHOLE else (0,)
+        return remote(here, there, send_sem.at[0], recv_sem.at[to], peer(link))
+
+    def landed(ref, sem):
+        pltpu.make_async_copy(ref, ref, sem).wait()
 
     swap = remote(st.at[pl.ds(hh * oz, hh)], kv.at[0, :, :, iz], x_sem.at[0], x_sem.at[1], {"cz": oz})
     q_swap = remote(q_hbm.at[:, pl.ds(hh * oz, hh)], qs.at[iz], x_sem.at[2], x_sem.at[3], {"cz": oz})
@@ -145,38 +146,39 @@
     row = lax.broadcasted_iota(jnp.int32, (16, w), 0)
     lead = lax.rem(lane, w // 2) // g - row
 
-    def attend(k, r0, r1):
+    def attend(units, r0, r1):
         first = r0 // 16
+        pieces = [(k, z) for k in units for z in range(2)]
 
         def scores(h, a):
             n = min(r1, 16 * (a + 1)) - r0
             q = jnp.concatenate([qt[h, a, 0], qt[h, a, 1]], axis=1)
-            keys = jnp.concatenate([kv[k, h, 0, z, r0:r0 + n] for z in range(2)], axis=0)
-            sc[h % 2, a, :2 * n] = jnp.dot(keys, q, preferred_element_type=jnp.float32)
+            keys = jnp.concatenate([kv[k, h, 0, z, r0:r0 + n] for k, z in pieces], axis=0)
+            sc[h % 2, a, :len(pieces) * n] = jnp.dot(keys, q, preferred_element_type=jnp.float32)
 
         def weigh(h):
             vis = []
-            for z in range(2):
+            for k, z in pieces:
                 gap = 2 * (chip - src[k, h]) - z
                 late = [jnp.where(gap + p >= 0, 0, 1) for p in range(2)]
                 vis.append(lead >= jnp.where(lane < w // 2, late[0], late[1]))
-            vt = kv[k, h, 1, :, r0:r1].reshape(2 * (r1 - r0), d).T
+            vt = jnp.concatenate([kv[k, h, 1, z, r0:r1] for k, z in pieces], axis=0).T
             for a in range(first, nb):
                 n = min(r1, 16 * (a + 1)) - r0
                 s = []
-                for z in range(2):
-                    x = sc[h % 2, a, z * n:(z + 1) * n]
+                for i in range(len(pieces)):
+                    x = sc[h % 2, a, i * n:(i + 1) * n]
                     if 16 * (a + 1) <= r1:
-                        edge = jnp.where(vis[z], x[n - 16:], NEG)
+                        edge = jnp.where(vis[i], x[n - 16:], NEG)
                         x = jnp.concatenate([x[:n - 16], edge], axis=0) if n > 16 else edge
                     s.append(x)
                 old = m_ref[h, a]
-                new = jnp.maximum(old, jnp.max(jnp.maximum(s[0], s[1]), axis=0, keepdims=True))
+                new = jnp.maximum(old, jnp.max(functools.reduce(jnp.maximum, s), axis=0, keepdims=True))
                 m_ref[h, a] = new
                 fade = jnp.exp2((old - new) * c)
                 top = new * c
                 e = [jnp.exp2(x * c - top) for x in s]
-                l_ref[h, a] = l_ref[h, a] * fade + jnp.sum((e[0] + e[1]).reshape(n // 8, 8, w), axis=0)
+                l_ref[h, a] = l_ref[h, a] * fade + jnp.sum(sum(e[1:], e[0]).reshape(n // 8, 8, w), axis=0)
                 weights = []
                 for x in e:
                     weights.append(x.astype(jnp.bfloat16))
@@ -193,58 +195,45 @@
                     scores(h + 1, a)
             weigh(h)
 
+    def out(h, rows):
+        return remote(ost.at[h, rows], o_ref.at[rows, hh * iz + h], out_sem.at[0], out_sem.at[1], {"cz": oz})
+
     def finish(a0, a1):
-        for h in range(hh):
+        @pl.loop(0, hh)
+        def _(h):
             for a in range(a0, a1):
-                o = acc[h, a] * (1.0 / jnp.sum(l_ref[h, a], axis=0, keepdims=True))
-                x = [o[:, p * 16 * g:(p + 1) * 16 * g].T.reshape(16, g, d).astype(jnp.bfloat16) for p in range(2)]
+                o = (acc[h, a] * (1.0 / jnp.sum(l_ref[h, a], axis=0, keepdims=True))).astype(jnp.bfloat16)
+                x = [o[:, p * 16 * g:(p + 1) * 16 * g].T.reshape(16, g, d) for p in range(2)]
                 here = iz == 0
-                ost[16 * a:16 * (a + 1), h] = jnp.where(here, x[1], x[0])
+                ost[h, 16 * a:16 * (a + 1)] = jnp.where(here, x[1], x[0])
                 o_ref[16 * a:16 * (a + 1), hh * iz + h] = jnp.where(here, x[0], x[1])
-
-    def out(n):
-        rows = (low, high)[n]
-        return remote(ost.at[rows], o_ref.at[rows, pl.ds(hh * iz, hh)], out_sem.at[0, n], out_sem.at[1, n], {"cz": oz})
-
-    tail = [(part, slot) for part in range(2) for slot in range(WHOLE, SLOTS)]
-    first = WHOLE - AHEAD + 1
-    late = {first: tail[:2], first + 1: tail[2:5], first + 2: tail[5:]}
-
-    def whole(k, carry):
+            out(h, slice(16 * a0, 16 * a1)).start()
+
+    def send_last(part):
+        for slot in range(WHOLE, SLOTS):
+            for n in range(4):
+                unit(n, slot, part).start()
+
+    def step(k, carry):
         for j in range(1, WHOLE + 1):
             @pl.when(k == j)
             def _():
-                for n in range(4):
-                    for part in parts(j - 1):
-                        unit(n, j - 1, part).wait_recv()
-                for n in range(4):
-                    if j >= 2:
-                        for part in parts(j - 2):
-                            unit(n, j - 2, part).wait_send()
+                landed(kv.at[j], recv_sem.at[j - 1])
                 if j - 1 + AHEAD < WHOLE:
                     for n in range(4):
                         unit(n, j - 1 + AHEAD).start()
-                for part, slot in late.get(j, ()):
-                    for n in range(4):
-                        unit(n, slot, part).start()
-        attend(k, 0, t)
+                if j - 1 + AHEAD == WHOLE:
+                    send_last(0)
+                if j - 1 + AHEAD == WHOLE + 1:
+                    @pl.when(iz == 0)
+                    def _():
+                        send_last(1)
+                if j == SLOTS - LAG:
+                    @pl.when(iz == 1)
+                    def _():
+                        send_last(1)
+        attend((k,), 0, t)
         return carry
-
-    def lows(k, carry):
-        for n in range(4):
-            land(n, k - 1, 0).wait_recv()
-        attend(k, 0, t // 2)
-        return carry
-
-    def highs(k, carry):
-        for n in range(4):
-            land(n, k - 1, 1).wait_recv()
-        attend(k, t // 2, t)
-        return carry
-
-    def land(n, slot, part):
-        piece = kv.at[1 + slot, n].at[:, :, (low, high)[part]]
-        return remote(piece, piece, send_sem.at[part, n, slot], recv_sem.at[part, n, slot], peer(LINKS[n]))
 
     for h in range(hh):
         src[0, h] = chip
@@ -252,21 +241,17 @@
         origin(slot)
     swap.wait_send()
     q_swap.wait_send()
-    lax.fori_loop(0, WHOLE + 1, whole, 0)
-    lax.fori_loop(WHOLE + 1, SLOTS + 1, lows, 0)
+    lax.fori_loop(0, WHOLE + 1, step, 0)
+    last = range(WHOLE + 1, SLOTS + 1)
+    landed(kv.at[pl.ds(WHOLE + 1, 2), :, :, :, low], recv_sem.at[WHOLE])
+    attend(last, 0, t // 2)
     finish(0, nb // 2)
-    out(0).start()
-    lax.fori_loop(WHOLE + 1, SLOTS + 1, highs, 0)
+    landed(kv.at[pl.ds(WHOLE + 1, 2), :, :, :, high], recv_sem.at[WHOLE + 1])
+    attend(last, t // 2, t)
     finish(nb // 2, nb)
-    out(1).start()
-    for n in range(4):
-        unit(n, WHOLE - 1).wait_send()
-        for slot in range(WHOLE, SLOTS):
-            for part in range(2):
-                unit(n, slot, part).wait_send()
-    for n in range(2):
-        out(n).wait_send()
-        out(n).wait_recv()
+    landed(kv.at[pl.ds(1, SLOTS)], send_sem.at[0])
+    landed(ost, out_sem.at[0])
+    landed(o_ref.at[:, pl.ds(hh * oz, hh)], out_sem.at[1])
 
 
 def solution(mesh):
@@ -296,14 +281,14 @@
                 pltpu.VMEM((hh, nb, d, w), jnp.float32),
                 pltpu.VMEM((hh, nb, 1, w), jnp.float32),
                 pltpu.VMEM((hh, nb, 8, w), jnp.float32),
-                pltpu.VMEM((t, hh, g, d), jnp.bfloat16),
+                pltpu.VMEM((hh, t, g, d), jnp.bfloat16),
                 pltpu.VMEM((2, nb, 2 * t, w), jnp.float32),
                 pltpu.SMEM((units, hh), jnp.int32),
                 pltpu.SemaphoreType.DMA((3,)),
                 pltpu.SemaphoreType.DMA((4,)),
-                pltpu.SemaphoreType.DMA((2, 4, SLOTS)),
-                pltpu.SemaphoreType.DMA((2, 4, SLOTS)),
-                pltpu.SemaphoreType.DMA((2, 2)),
+                pltpu.SemaphoreType.DMA((1,)),
+                pltpu.SemaphoreType.DMA((SLOTS,)),
+                pltpu.SemaphoreType.DMA((2,)),
             ],
             compiler_params=pltpu.CompilerParams(collective_id=0, has_side_effects=True, vmem_limit_bytes=20 << 20),
         )(*(pltpu.with_memory_space_constraint(x, pltpu.HBM) for x in (k, v, q.reshape(t, hkv, g, d))))

time: 36.6 us -> 34.3 us (0.937)
  Pallas kernels: 35.6 us -> 33.2 us
    pallas_call x1, Pallas kernels: 35.6 us -> 33.2 us  [local(): pl.pallas_call(_kernel, out_shape=jax.ShapeDtypeStruct((t, hkv, g, d), jn...]
where the time goes in v7:
time: 34.3 us; the launch traced here: 34.2 us
  Pallas kernels  33.2 us (97%)
  local copies, waits for them, and re-layouts  0.97 us (3%)
    pallas_call x1, Pallas kernels, local(): pl.pallas_call(_kernel, out_shape=jax.ShapeDtypeStruct((t, hkv, g, d), jn...  33.2 us
    unnamed x1, local copies, waits for them, and re-layouts  0.97 us

profile of v7, /device:TPU:97, one launch (start us, length us, event | category | flops | bytes accessed | tf_op | source)
XLA Modules:
  0.0 34.2 jit_solution(16598751150261935472)
XLA Ops:
  0.0 33.2 %shard_map.37 = bf16[64,8,8,128]{3,2,1,0:T(8,128)(2,1)S(1)} custom-call(bf16[64,8,128]{2,1,0:T(8,128)(2,1)} %k_hbm.1, bf16[64,8,128]{2,1,0:T(8,128)(2,1)} %v_hbm.1, bf16[64,8,8,128]{3,2,1,0:T(8,128)(2,1)} %bitcast.3), custom_call_target="tpu_custom_call" | custom-call | tf_op jit(solution)/shard_map/pallas_call | solution.py:269
  33.2 1.0 %copy.5 = bf16[64,64,128]{2,1,0:T(8,128)(2,1)} copy(bf16[64,64,128]{2,1,0:T(8,128)(2,1)S(1)} %bitcast.2) | data formatting | bytes 2097152

commit v8 on v7

--- a/solution.py
+++ b/solution.py
@@ -146,7 +146,7 @@
     row = lax.broadcasted_iota(jnp.int32, (16, w), 0)
     lead = lax.rem(lane, w // 2) // g - row
 
-    def attend(units, r0, r1):
+    def attend(units, r0, r1, ahead=2):
         first = r0 // 16
         pieces = [(k, z) for k in units for z in range(2)]
 
@@ -154,7 +154,7 @@
             n = min(r1, 16 * (a + 1)) - r0
             q = jnp.concatenate([qt[h, a, 0], qt[h, a, 1]], axis=1)
             keys = jnp.concatenate([kv[k, h, 0, z, r0:r0 + n] for k, z in pieces], axis=0)
-            sc[h % 2, a, :len(pieces) * n] = jnp.dot(keys, q, preferred_element_type=jnp.float32)
+            sc[h, a, :len(pieces) * n] = jnp.dot(keys, q, preferred_element_type=jnp.float32)
 
         def weigh(h):
             vis = []
@@ -167,7 +167,7 @@
                 n = min(r1, 16 * (a + 1)) - r0
                 s = []
                 for i in range(len(pieces)):
-                    x = sc[h % 2, a, i * n:(i + 1) * n]
+                    x = sc[h, a, i * n:(i + 1) * n]
                     if 16 * (a + 1) <= r1:
                         edge = jnp.where(vis[i], x[n - 16:], NEG)
                         x = jnp.concatenate([x[:n - 16], edge], axis=0) if n > 16 else edge
@@ -187,13 +187,12 @@
                 pv = jnp.dot(vt, jnp.concatenate(weights, axis=0), preferred_element_type=jnp.float32)
                 acc[h, a] = acc[h, a] * fade + pv
 
-        for a in range(first, nb):
-            scores(0, a)
-        for h in range(hh):
-            if h + 1 < hh:
+        for i in range(hh + ahead):
+            if i < hh:
                 for a in range(first, nb):
-                    scores(h + 1, a)
-            weigh(h)
+                    scores(i, a)
+            if i >= ahead:
+                weigh(i - ahead)
 
     def out(h, rows):
         return remote(ost.at[h, rows], o_ref.at[rows, hh * iz + h], out_sem.at[0], out_sem.at[1], {"cz": oz})
@@ -247,7 +246,7 @@
     attend(last, 0, t // 2)
     finish(0, nb // 2)
     landed(kv.at[pl.ds(WHOLE + 1, 2), :, :, :, high], recv_sem.at[WHOLE + 1])
-    attend(last, t // 2, t)
+    attend(last, t // 2, t, 2)
     finish(nb // 2, nb)
     landed(kv.at[pl.ds(1, SLOTS)], send_sem.at[0])
     landed(ost, out_sem.at[0])
@@ -282,7 +281,7 @@
                 pltpu.VMEM((hh, nb, 1, w), jnp.float32),
                 pltpu.VMEM((hh, nb, 8, w), jnp.float32),
                 pltpu.VMEM((hh, t, g, d), jnp.bfloat16),
-                pltpu.VMEM((2, nb, 2 * t, w), jnp.float32),
+                pltpu.VMEM((hh, nb, 2 * t, w), jnp.float32),
                 pltpu.SMEM((units, hh), jnp.int32),
                 pltpu.SemaphoreType.DMA((3,)),
                 pltpu.SemaphoreType.DMA((4,)),

time: 34.3 us -> 34.1 us (level)
  no operation moved by 1% of the time
where the time goes in v8:
time: 34.1 us; the launch traced here: 34 us
  Pallas kernels  33 us (97%)
  local copies, waits for them, and re-layouts  0.97 us (3%)
    pallas_call x1, Pallas kernels, local(): pl.pallas_call(_kernel, out_shape=jax.ShapeDtypeStruct((t, hkv, g, d), jn...  33 us
    unnamed x1, local copies, waits for them, and re-layouts  0.97 us

profile of v8, /device:TPU:97, one launch (start us, length us, event | category | flops | bytes accessed | tf_op | source)
XLA Modules:
  0.0 34.0 jit_solution(9486496775864820946)
XLA Ops:
  0.0 33.0 %shard_map.37 = bf16[64,8,8,128]{3,2,1,0:T(8,128)(2,1)S(1)} custom-call(bf16[64,8,128]{2,1,0:T(8,128)(2,1)} %k_hbm.1, bf16[64,8,128]{2,1,0:T(8,128)(2,1)} %v_hbm.1, bf16[64,8,8,128]{3,2,1,0:T(8,128)(2,1)} %bitcast.3), custom_call_target="tpu_custom_call" | custom-call | tf_op jit(solution)/shard_map/pallas_call | solution.py:268
  33.1 1.0 %copy.5 = bf16[64,64,128]{2,1,0:T(8,128)(2,1)} copy(bf16[64,64,128]{2,1,0:T(8,128)(2,1)S(1)} %bitcast.2) | data formatting | bytes 2097152

commit v9 on v8

--- a/solution.py
+++ b/solution.py
@@ -18,6 +18,7 @@
 )
 SLOTS = len(PLAN)
 AHEAD = 4
+RECVS = 2 * AHEAD
 WHOLE = SLOTS - 2
 LAG = 2
 
@@ -81,8 +82,6 @@
         copy.wait()
         x = jnp.swapaxes(ref[...].astype(jnp.float32), 0, 1)
         st[:, n] = x.astype(jnp.bfloat16)
-    for h in range(hh):
-        kv[0, h, :, iz] = st[hh * iz + h]
 
     def remote(a, b, s, r, to):
         return pltpu.make_async_remote_copy(
@@ -99,7 +98,7 @@
         elif slot >= WHOLE:
             rows, to = (low, high)[part], WHOLE + part
             here, there = here.at[:, :, rows], there.at[:, :, rows]
-        return remote(here, there, send_sem.at[0], recv_sem.at[to], peer(link))
+        return remote(here, there, send_sem.at[0], recv_sem.at[to % RECVS], peer(link))
 
     def landed(ref, sem):
         pltpu.make_async_copy(ref, ref, sem).wait()
@@ -108,10 +107,13 @@
     q_swap = remote(q_hbm.at[:, pl.ds(hh * oz, hh)], qs.at[iz], x_sem.at[2], x_sem.at[3], {"cz": oz})
 
     pl.semaphore_wait(barrier, len(LINKS) + 1)
+    for n in range(4):
+        unit(n, 0).start()
     swap.start()
-    for slot in range(2):
-        for n in range(4):
-            unit(n, slot).start()
+    for n in range(4):
+        unit(n, 1).start()
+    for h in range(hh):
+        kv[0, h, :, iz] = st[hh * iz + h]
     q_swap.start()
     swap.wait_recv()
     for slot in range(2):
@@ -217,7 +219,7 @@
         for j in range(1, WHOLE + 1):
             @pl.when(k == j)
             def _():
-                landed(kv.at[j], recv_sem.at[j - 1])
+                landed(kv.at[j], recv_sem.at[(j - 1) % RECVS])
                 if j - 1 + AHEAD < WHOLE:
                     for n in range(4):
                         unit(n, j - 1 + AHEAD).start()
@@ -242,10 +244,10 @@
     q_swap.wait_send()
     lax.fori_loop(0, WHOLE + 1, step, 0)
     last = range(WHOLE + 1, SLOTS + 1)
-    landed(kv.at[pl.ds(WHOLE + 1, 2), :, :, :, low], recv_sem.at[WHOLE])
+    landed(kv.at[pl.ds(WHOLE + 1, 2), :, :, :, low], recv_sem.at[WHOLE % RECVS])
     attend(last, 0, t // 2)
     finish(0, nb // 2)
-    landed(kv.at[pl.ds(WHOLE + 1, 2), :, :, :, high], recv_sem.at[WHOLE + 1])
+    landed(kv.at[pl.ds(WHOLE + 1, 2), :, :, :, high], recv_sem.at[(WHOLE + 1) % RECVS])
     attend(last, t // 2, t, 2)
     finish(nb // 2, nb)
     landed(kv.at[pl.ds(1, SLOTS)], send_sem.at[0])
@@ -286,7 +288,7 @@
                 pltpu.SemaphoreType.DMA((3,)),
                 pltpu.SemaphoreType.DMA((4,)),
                 pltpu.SemaphoreType.DMA((1,)),
-                pltpu.SemaphoreType.DMA((SLOTS,)),
+                pltpu.SemaphoreType.DMA((RECVS,)),
                 pltpu.SemaphoreType.DMA((2,)),
             ],
             compiler_params=pltpu.CompilerParams(collective_id=0, has_side_effects=True, vmem_limit_bytes=20 << 20),

time: 34.1 us -> 34.1 us (level)
  no operation moved by 1% of the time
where the time goes in v9:
time: 34.1 us; the launch traced here: 34 us
  Pallas kernels  33 us (97%)
  local copies, waits for them, and re-layouts  0.97 us (3%)
    pallas_call x1, Pallas kernels, local(): pl.pallas_call(_kernel, out_shape=jax.ShapeDtypeStruct((t, hkv, g, d), jn...  33 us
    unnamed x1, local copies, waits for them, and re-layouts  0.97 us

profile of v9, /device:TPU:97, one launch (start us, length us, event | category | flops | bytes accessed | tf_op | source)
XLA Modules:
  0.0 34.0 jit_solution(7710322549021777747)
XLA Ops:
  0.0 33.0 %shard_map.37 = bf16[64,8,8,128]{3,2,1,0:T(8,128)(2,1)S(1)} custom-call(bf16[64,8,128]{2,1,0:T(8,128)(2,1)} %k_hbm.1, bf16[64,8,128]{2,1,0:T(8,128)(2,1)} %v_hbm.1, bf16[64,8,8,128]{3,2,1,0:T(8,128)(2,1)} %bitcast.3), custom_call_target="tpu_custom_call" | custom-call | tf_op jit(solution)/shard_map/pallas_call | solution.py:270
  33.0 1.0 %copy.5 = bf16[64,64,128]{2,1,0:T(8,128)(2,1)} copy(bf16[64,64,128]{2,1,0:T(8,128)(2,1)S(1)} %bitcast.2) | data formatting | bytes 2097152

commit v10 on v9

--- a/solution.py
+++ b/solution.py
@@ -199,16 +199,18 @@
     def out(h, rows):
         return remote(ost.at[h, rows], o_ref.at[rows, hh * iz + h], out_sem.at[0], out_sem.at[1], {"cz": oz})
 
-    def finish(a0, a1):
-        @pl.loop(0, hh)
-        def _(h):
-            for a in range(a0, a1):
-                o = (acc[h, a] * (1.0 / jnp.sum(l_ref[h, a], axis=0, keepdims=True))).astype(jnp.bfloat16)
-                x = [o[:, p * 16 * g:(p + 1) * 16 * g].T.reshape(16, g, d) for p in range(2)]
-                here = iz == 0
-                ost[h, 16 * a:16 * (a + 1)] = jnp.where(here, x[1], x[0])
-                o_ref[16 * a:16 * (a + 1), hh * iz + h] = jnp.where(here, x[0], x[1])
-            out(h, slice(16 * a0, 16 * a1)).start()
+    def finish(a0, a1, together):
+        @pl.loop(0, hh // together)
+        def _(i):
+            for h in [i * together + n for n in range(together)]:
+                for a in range(a0, a1):
+                    o = (acc[h, a] * (1.0 / jnp.sum(l_ref[h, a], axis=0, keepdims=True))).astype(jnp.bfloat16)
+                    x = [o[:, p * 16 * g:(p + 1) * 16 * g].T.reshape(16, g, d) for p in range(2)]
+                    here = iz == 0
+                    ost[h, 16 * a:16 * (a + 1)] = jnp.where(here, x[1], x[0])
+                    o_ref[16 * a:16 * (a + 1), hh * iz + h] = jnp.where(here, x[0], x[1])
+            for h in [i * together + n for n in range(together)]:
+                out(h, slice(16 * a0, 16 * a1)).start()
 
     def send_last(part):
         for slot in range(WHOLE, SLOTS):
@@ -246,10 +248,10 @@
     last = range(WHOLE + 1, SLOTS + 1)
     landed(kv.at[pl.ds(WHOLE + 1, 2), :, :, :, low], recv_sem.at[WHOLE % RECVS])
     attend(last, 0, t // 2)
-    finish(0, nb // 2)
+    finish(0, nb // 2, 2)
     landed(kv.at[pl.ds(WHOLE + 1, 2), :, :, :, high], recv_sem.at[(WHOLE + 1) % RECVS])
     attend(last, t // 2, t, 2)
-    finish(nb // 2, nb)
+    finish(nb // 2, nb, 1)
     landed(kv.at[pl.ds(1, SLOTS)], send_sem.at[0])
     landed(ost, out_sem.at[0])
     landed(o_ref.at[:, pl.ds(hh * oz, hh)], out_sem.at[1])

time: 34.1 us -> 33.9 us (level)
  no operation moved by 1% of the time
where the time goes in v10:
time: 33.9 us; the launch traced here: 33.8 us
  Pallas kernels  32.9 us (97%)
  local copies, waits for them, and re-layouts  0.97 us (3%)
    pallas_call x1, Pallas kernels, local(): pl.pallas_call(_kernel, out_shape=jax.ShapeDtypeStruct((t, hkv, g, d), jn...  32.9 us
    unnamed x1, local copies, waits for them, and re-layouts  0.97 us

profile of v10, /device:TPU:97, one launch (start us, length us, event | category | flops | bytes accessed | tf_op | source)
XLA Modules:
  0.0 33.8 jit_solution(9106641902571752217)
XLA Ops:
  0.0 32.9 %shard_map.37 = bf16[64,8,8,128]{3,2,1,0:T(8,128)(2,1)S(1)} custom-call(bf16[64,8,128]{2,1,0:T(8,128)(2,1)} %k_hbm.1, bf16[64,8,128]{2,1,0:T(8,128)(2,1)} %v_hbm.1, bf16[64,8,8,128]{3,2,1,0:T(8,128)(2,1)} %bitcast.3), custom_call_target="tpu_custom_call" | custom-call | tf_op jit(solution)/shard_map/pallas_call | solution.py:272
  32.9 1.0 %copy.5 = bf16[64,64,128]{2,1,0:T(8,128)(2,1)} copy(bf16[64,64,128]{2,1,0:T(8,128)(2,1)S(1)} %bitcast.2) | data formatting | bytes 2097152

commit v11 on v10

--- a/solution.py
+++ b/solution.py
@@ -248,7 +248,7 @@
     last = range(WHOLE + 1, SLOTS + 1)
     landed(kv.at[pl.ds(WHOLE + 1, 2), :, :, :, low], recv_sem.at[WHOLE % RECVS])
     attend(last, 0, t // 2)
-    finish(0, nb // 2, 2)
+    finish(0, nb // 2, 4)
     landed(kv.at[pl.ds(WHOLE + 1, 2), :, :, :, high], recv_sem.at[(WHOLE + 1) % RECVS])
     attend(last, t // 2, t, 2)
     finish(nb // 2, nb, 1)

time: 33.9 us -> 33.8 us (level)
  no operation moved by 1% of the time
where the time goes in v11:
time: 33.8 us; the launch traced here: 33.7 us
  Pallas kernels  32.7 us (97%)
  local copies, waits for them, and re-layouts  0.97 us (3%)
    pallas_call x1, Pallas kernels, local(): pl.pallas_call(_kernel, out_shape=jax.ShapeDtypeStruct((t, hkv, g, d), jn...  32.7 us
    unnamed x1, local copies, waits for them, and re-layouts  0.97 us

profile of v11, /device:TPU:97, one launch (start us, length us, event | category | flops | bytes accessed | tf_op | source)
XLA Modules:
  0.0 33.7 jit_solution(104325240292865812)
XLA Ops:
  0.0 32.7 %shard_map.37 = bf16[64,8,8,128]{3,2,1,0:T(8,128)(2,1)S(1)} custom-call(bf16[64,8,128]{2,1,0:T(8,128)(2,1)} %k_hbm.1, bf16[64,8,128]{2,1,0:T(8,128)(2,1)} %v_hbm.1, bf16[64,8,8,128]{3,2,1,0:T(8,128)(2,1)} %bitcast.3), custom_call_target="tpu_custom_call" | custom-call | tf_op jit(solution)/shard_map/pallas_call | solution.py:272
  32.7 1.0 %copy.5 = bf16[64,64,128]{2,1,0:T(8,128)(2,1)} copy(bf16[64,64,128]{2,1,0:T(8,128)(2,1)S(1)} %bitcast.2) | data formatting | bytes 2097152

commit v12 on v11

--- a/solution.py
+++ b/solution.py
@@ -104,7 +104,7 @@
         pltpu.make_async_copy(ref, ref, sem).wait()
 
     swap = remote(st.at[pl.ds(hh * oz, hh)], kv.at[0, :, :, iz], x_sem.at[0], x_sem.at[1], {"cz": oz})
-    q_swap = remote(q_hbm.at[:, pl.ds(hh * oz, hh)], qs.at[iz], x_sem.at[2], x_sem.at[3], {"cz": oz})
+    q_swap = remote(q_hbm.at[:, pl.ds(hh * oz, hh)], qs.at[iz], out_sem.at[0], in_sem.at[2], {"cz": oz})
 
     pl.semaphore_wait(barrier, len(LINKS) + 1)
     for n in range(4):
@@ -134,8 +134,7 @@
                 x = qs[p, 16 * a:16 * (a + 1), h].astype(jnp.float32).reshape(16 * g, d)
                 qt[h, a, p] = x.T.astype(jnp.bfloat16)
 
-    q_in.wait()
-    q_swap.wait_recv()
+    landed(qs, in_sem.at[2])
     for p in range(2):
         turn(p)
 
@@ -243,7 +242,6 @@
     for slot in range(SLOTS):
         origin(slot)
     swap.wait_send()
-    q_swap.wait_send()
     lax.fori_loop(0, WHOLE + 1, step, 0)
     last = range(WHOLE + 1, SLOTS + 1)
     landed(kv.at[pl.ds(WHOLE + 1, 2), :, :, :, low], recv_sem.at[WHOLE % RECVS])
@@ -253,7 +251,7 @@
     attend(last, t // 2, t, 2)
     finish(nb // 2, nb, 1)
     landed(kv.at[pl.ds(1, SLOTS)], send_sem.at[0])
-    landed(ost, out_sem.at[0])
+    landed(o_ref, out_sem.at[0])
     landed(o_ref.at[:, pl.ds(hh * oz, hh)], out_sem.at[1])
 
 
@@ -288,7 +286,7 @@
                 pltpu.VMEM((hh, nb, 2 * t, w), jnp.float32),
                 pltpu.SMEM((units, hh), jnp.int32),
                 pltpu.SemaphoreType.DMA((3,)),
-                pltpu.SemaphoreType.DMA((4,)),
+                pltpu.SemaphoreType.DMA((2,)),
                 pltpu.SemaphoreType.DMA((1,)),
                 pltpu.SemaphoreType.DMA((RECVS,)),
                 pltpu.SemaphoreType.DMA((2,)),

time: 33.8 us -> 33.8 us (level)
  no operation moved by 1% of the time
where the time goes in v12:
time: 33.8 us; the launch traced here: 33.7 us
  Pallas kernels  32.7 us (97%)
  local copies, waits for them, and re-layouts  0.97 us (3%)
    pallas_call x1, Pallas kernels, local(): pl.pallas_call(_kernel, out_shape=jax.ShapeDtypeStruct((t, hkv, g, d), jn...  32.7 us
    unnamed x1, local copies, waits for them, and re-layouts  0.97 us

profile of v12, /device:TPU:97, one launch (start us, length us, event | category | flops | bytes accessed | tf_op | source)
XLA Modules:
  0.0 33.7 jit_solution(17791141143768610648)
XLA Ops:
  0.0 32.7 %shard_map.37 = bf16[64,8,8,128]{3,2,1,0:T(8,128)(2,1)S(1)} custom-call(bf16[64,8,128]{2,1,0:T(8,128)(2,1)} %k_hbm.1, bf16[64,8,128]{2,1,0:T(8,128)(2,1)} %v_hbm.1, bf16[64,8,8,128]{3,2,1,0:T(8,128)(2,1)} %bitcast.3), custom_call_target="tpu_custom_call" | custom-call | tf_op jit(solution)/shard_map/pallas_call | solution.py:270
  32.7 1.0 %copy.5 = bf16[64,64,128]{2,1,0:T(8,128)(2,1)} copy(bf16[64,64,128]{2,1,0:T(8,128)(2,1)S(1)} %bitcast.2) | data formatting | bytes 2097152
